TPU v7x, 768 devices: a whole 4x8x12 slice. The times are simulated.
768 devices in a mesh: dp: 96 (over z, x, core), mp: 8 (over y).
Axes of the slice: x: 4, y: 8, z: 12, core: 2. Of those that a mesh axis runs over, the one named last changes fastest.
Arguments:
- vision_rows: bfloat16 [24576, 1024], P('dp'), may hold values from -6 to 6
- image_count: int32 [768], P('dp'), may hold values from 0 to 4
- proj_flat: bfloat16 [36864, 128], P(('dp', 'mp')), may hold values from -0.1875 to 0.1875
- text_embeds: bfloat16 [73728, 4096], P(('dp', 'mp')), may hold values from -6 to 6
- norm_gain: float32 [4096], replicated, may hold values from 0.1 to 1.9
- q_weight: bfloat16 [4096, 4096], P(None, 'mp'), may hold values from -0.09375 to 0.09375
- q_grad: bfloat16 [98304, 4096], P('dp', 'mp'), may hold values from -6 to 6
Outputs:
- text_grad: bfloat16 [73728, 4096], P(('dp', 'mp'))
- proj_grad: float32 [36864, 128], P(('dp', 'mp'))
Inputs may be any that keep to these rules, and one draw needn't show every extreme that they name: Slot s of device k holds an image when s < image_count[k]; other slots are padding.
All inputs are finite; a program needn't handle non-finite values.
Results may differ from a plain program's by a relative error of at most 0.014.
Values may be sent and summed in bfloat16 or wider, within the bound.
A program may use at most 64 MiB of HBM per device.

v0:
```python
import jax
import jax.numpy as jnp
from jax import lax
from jax.sharding import Mesh
from jax.sharding import PartitionSpec as P

IMG_MAX = 4
PATCH = 8
DP = ("dp_0", "dp_1", "dp_2")
DP_MP = ("dp_0", "dp_1", "dp_2", "mp")


norm_eps = 1e-05


def own_block(blocks, axes, sequence):
    dims = [lax.axis_size(a) for a in axes]
    blocks = blocks.reshape(*dims, *blocks.shape[1:])
    blocks = blocks.transpose(*sequence, *range(len(axes), blocks.ndim))
    blocks = blocks.reshape(-1, *blocks.shape[len(axes) :])
    for k in sequence:
        blocks = lax.psum_scatter(blocks, axes[k], scatter_dimension=0, tiled=True)
    return blocks[0]


def in_blocks(array, dim, count):
    dims = array.shape
    blocks = array.reshape(*dims[:dim], count, dims[dim] // count, *dims[dim + 1 :])
    return jnp.moveaxis(blocks, dim, 0)


def summed_rows(array, axes, sequence, dim):
    count = lax.axis_size(axes)
    return own_block(in_blocks(array, dim, count), axes, sequence)


def row_term(left, weight):
    return lax.dot_general(
        left, weight, (((1,), (1,)), ((), ())), preferred_element_type=jnp.float32
    )


def norm_back(rows_in, grads, gain):
    inputs = rows_in.astype(jnp.float32)
    inv_rms = lax.rsqrt(jnp.mean(inputs * inputs, axis=-1, keepdims=True) + norm_eps)
    scaled = gain[None, :] * grads
    inner_mean = jnp.mean(scaled * inputs, axis=-1, keepdims=True)
    return inv_rms * scaled - inputs * inv_rms**3 * inner_mean


def body(vision_rows, image_count, proj_flat, text_embeds, norm_gain, q_weight, q_grad):
    groups = lax.axis_size("mp")
    member = lax.axis_index("mp")
    shards = lax.axis_size(DP)
    enc_width = vision_rows.shape[1]
    block_cols = q_weight.shape[1]
    used_count = enc_width * block_cols
    image_rows = IMG_MAX * PATCH
    gathered = lax.all_gather(proj_flat, DP, axis=0, tiled=True)
    proj_block = gathered.reshape(-1)[:used_count].reshape(enc_width, block_cols)
    embed_cols = jnp.dot(vision_rows, proj_block, preferred_element_type=jnp.float32).astype(
        jnp.bfloat16
    )
    row_ids = jnp.arange(groups * image_rows, dtype=jnp.int32)
    owners = row_ids // image_rows
    slot_ids = row_ids % image_rows // PATCH
    owner_match = owners[:, None] == jnp.arange(groups, dtype=jnp.int32)[None, :]
    owner_counts = jnp.sum(jnp.where(owner_match, image_count[None, :], 0), axis=1)
    live_group = (slot_ids < owner_counts)[:, None]
    norm_grad = lax.psum_scatter(
        row_term(q_grad, q_weight).astype(jnp.bfloat16), "mp", scatter_dimension=0, tiled=True
    ).astype(jnp.float32)
    embed_own = lax.all_to_all(embed_cols, "mp", split_axis=0, concat_axis=1, tiled=True)
    decoder_in = jnp.concatenate([embed_own, text_embeds], axis=0)
    input_grad = norm_back(decoder_in, norm_grad, norm_gain)
    own_live = lax.dynamic_slice_in_dim(live_group, member * image_rows, image_rows, 0)
    image_own = jnp.where(own_live, input_grad[:image_rows], 0.0).astype(jnp.bfloat16)
    image_cols = lax.all_to_all(image_own, "mp", split_axis=1, concat_axis=0, tiled=True)
    text_grad = input_grad[image_rows:].astype(jnp.bfloat16)
    grad_scale = 1.0 / jnp.sqrt(jnp.float32(shards * groups * image_rows))
    proj_part = (
        lax.dot_general(
            vision_rows, image_cols, (((0,), (0,)), ((), ())), preferred_element_type=jnp.float32
        )
        * grad_scale
    )
    stored_rows = proj_flat.shape[0]
    padded = jnp.pad(proj_part.reshape(-1), (0, shards * stored_rows * 128 - used_count))
    padded = padded.reshape(shards * stored_rows, 128)
    proj_grad = summed_rows(padded, DP, (2, 1, 0), 0)
    return (text_grad, proj_grad)


def solution(mesh):
    finer = Mesh(mesh.devices.reshape(12, 4, 2, mesh.shape["mp"]), ("dp_0", "dp_1", "dp_2", "mp"))
    placed = (P(DP, None), P(DP), P(DP_MP, None), P(DP_MP, None), P(), P(None, "mp"), P(DP, "mp"))
    return jax.shard_map(
        body,
        mesh=finer,
        in_specs=placed,
        out_specs=(P(DP_MP, None), P(DP_MP, None)),
        check_vma=False,
    )
```

profile of v0, /device:TPU:2, one launch (start us, length us, event | category | flops | bytes accessed | tf_op | source)
XLA Modules:
  0.0 299.2 jit_solution(3021089597602194798)
XLA Ops:
  8.0 0.0 all-gather.2.cloned.1.call-start
  8.1 0.7 all-gather.2.cloned.1.call-update
  8.7 0.0 reduce-scatter.5.cloned.1.call-start
  8.8 0.4 copy-done
  9.2 8.9 %convolution_convert_fusion = bf16[1024,4096]{1,0:T(8,128)(2,1)} fusion(bf16[1024,512]{1,0:T(8,128)(2,1)S(1)} %copy-done, bf16[4096,512]{1,0:T(8,128)(2,1)} %param.12), kind=kOutput, calls=%fused_computation | convolution fusion | flops 4299161600 | bytes 13631488 | tf_op jit(solution)/shard_map/dot_general | solution.py:38
  18.2 0.0 reduce-scatter.5.cloned.1.call-update
  18.2 116.7 %all-gather.2.cloned.1.call-done = bf16[4608,128]{1,0:T(8,128)(2,1)} async-done(((bf16[48,128]{1,0:T(8,128)(2,1)}), bf16[4608,128]{1,0:T(8,128)(2,1)}) %all-gather.2.cloned.1.call-update) | async-done | bytes 1179664 | tf_op jit(solution)/shard_map/all_gather | solution.py:59
  134.8 1.2 slice-done
  136.1 0.6 reshape.57
  136.7 2.3 convolution_convert_fusion.1
  139.0 6.7 %all-to-all-start = ((bf16[8,32,512]{2,1,0:T(8,128)(2,1)}), bf16[8,32,512]{2,1,0:T(8,128)(2,1)S(1)}, u32[]{:S(2)}, u32[]{:S(2)}) async-start(bf16[8,32,512]{2,1,0:T(8,128)(2,1)} %bitcast), calls=%async_computation | async-start | bytes 524288 | tf_op jit(solution)/shard_map/all_to_all | solution.py:73
  145.7 0.0 reduce-scatter.7.cloned.1.call-start
  145.8 0.1 select_reduce_fusion
  145.9 0.1 dynamic-slice.3
  146.0 12.0 %all-to-all-done = bf16[8,32,512]{2,1,0:T(8,128)(2,1)S(1)} async-done(((bf16[8,32,512]{2,1,0:T(8,128)(2,1)}), bf16[8,32,512]{2,1,0:T(8,128)(2,1)S(1)}, u32[]{:S(2)}, u32[]{:S(2)}) %all-to-all-start) | async-done | bytes 262176 | tf_op jit(solution)/shard_map/all_to_all | solution.py:73
  158.0 0.0 reduce-scatter.5.cloned.1.call-done
  158.1 1.9 fusion
  160.0 0.7 fusion.2
  160.8 0.1 fusion.4
  160.9 14.1 %all_to_all.38 = bf16[32,8,512]{2,0,1:T(8,128)(2,1)S(1)} all-to-all(bf16[32,8,512]{2,0,1:T(8,128)(2,1)S(1)} %bitcast.34), channel_id=1, replica_groups=mesh['dp_0'=12,'dp_1'=4,'dp_2'=2,'mp'=8] {'mp'}, dimensions={1} | all-to-all | bytes 524288 | tf_op jit(solution)/shard_map/all_to_all | solution.py:78
  175.0 0.5 multiply_bitcast_fusion
  175.5 1.9 copy.19
  177.4 2.1 copy.23
  179.5 0.2 pad.4
  179.6 1.6 copy.20
  181.3 0.0 reduce-scatter.7.cloned.1.call-update
  181.3 0.0 reduce-scatter.9.cloned.1.call-start
  181.3 13.2 %reduce-scatter.7.cloned.1.call-done = f32[48,48,128]{2,1,0:T(8,128)} async-done(((f32[96,48,128]{2,1,0:T(8,128)}), f32[48,48,128]{2,1,0:T(8,128)}) %reduce-scatter.7.cloned.1.call-update) | async-done | bytes 1179664 | tf_op jit(solution)/shard_map/reduce_scatter | solution.py:22
  194.6 0.0 reduce-scatter.11.cloned.1.call-start
  194.7 35.4 %reduce-scatter.9.cloned.1.call-done = f32[12,48,128]{2,1,0:T(8,128)} async-done(((f32[48,48,128]{2,1,0:T(8,128)}), f32[12,48,128]{2,1,0:T(8,128)}) %reduce-scatter.9.cloned.1.call-update) | async-done | bytes 294928 | tf_op jit(solution)/shard_map/reduce_scatter | solution.py:22
  230.1 0.9 slice.21
  231.0 61.1 %reduce-scatter.11.cloned.1.call-done = f32[1,48,128]{2,1,0:T(8,128)} async-done(((f32[12,48,128]{2,1,0:T(8,128)}), f32[1,48,128]{2,1,0:T(8,128)}) %reduce-scatter.11.cloned.1.call-update) | async-done | bytes 24592 | tf_op jit(solution)/shard_map/reduce_scatter | solution.py:22
  (23 shorter events, 0.1 us)
Async XLA Ops:
  8.0 1.2 copy-start
  8.0 126.8 %all-gather.2.cloned.1.call-start = ((), (), s32[]{:S(2)}) async-start(), calls=%async_computation.6 | async-start | bytes 1191936 | tf_op jit(solution)/shard_map/all_gather | solution.py:59
  8.7 149.3 %reduce-scatter.5.cloned.1.call-start = ((), (), s32[]{:S(2)}) async-start(), calls=%async_computation.7 | async-start | bytes 9437184 | tf_op jit(solution)/shard_map/reduce_scatter | solution.py:70
  134.8 1.2 slice-start
  136.1 9.7 %copy-start.7 = (s32[8]{0:T(128)S(1)}, s32[8]{0:T(128)}, u32[]{:S(2)}) copy-start(s32[8]{0:T(128)} %param.8) | copy-start | bytes 100
  136.1 22.0 %copy-start.6 = (f32[4096]{0:T(1024)S(1)}, f32[4096]{0:T(1024)}, u32[]{:S(2)}) copy-start(f32[4096]{0:T(1024)} %param.11) | copy-start | bytes 49156
  136.7 21.3 %copy-start.4 = (bf16[96,4096]{1,0:T(8,128)(2,1)S(1)}, bf16[96,4096]{1,0:T(8,128)(2,1)}, u32[]{:S(2)}) copy-start(bf16[96,4096]{1,0:T(8,128)(2,1)} %param.10) | copy-start | bytes 2359300
  139.0 19.0 %all-to-all-start = ((bf16[8,32,512]{2,1,0:T(8,128)(2,1)}), bf16[8,32,512]{2,1,0:T(8,128)(2,1)S(1)}, u32[]{:S(2)}, u32[]{:S(2)}) async-start(bf16[8,32,512]{2,1,0:T(8,128)(2,1)} %bitcast), calls=%async_computation | async-start | bytes 524288 | tf_op jit(solution)/shard_map/all_to_all | solution.py:73
  145.7 48.8 %reduce-scatter.7.cloned.1.call-start = ((), (), s32[]{:S(2)}) async-start(), calls=%async_computation.8 | async-start | bytes 3538944 | tf_op jit(solution)/shard_map/reduce_scatter | solution.py:22
  158.1 1.9 copy-start.3
  160.0 15.0 %copy-start.5 = (bf16[256,1024]{1,0:T(8,128)(2,1)S(1)}, bf16[256,1024]{1,0:T(8,128)(2,1)}, u32[]{:S(2)}) copy-start(bf16[256,1024]{1,0:T(8,128)(2,1)} %param.7) | copy-start | bytes 1572868
  160.7 14.3 %copy-start.1 = (bf16[128,4096]{1,0:T(8,128)(2,1)}, bf16[128,4096]{1,0:T(8,128)(2,1)S(1)}, u32[]{:S(2)}) copy-start(bf16[128,4096]{1,0:T(8,128)(2,1)S(1)} %fusion.2) | copy-start | bytes 3145732
  181.3 48.8 %copy-start.2 = (bf16[128,4096]{1,0:T(8,128)(2,1)S(1)}, bf16[128,4096]{1,0:T(8,128)(2,1)}, u32[]{:S(2)}) copy-start(bf16[128,4096]{1,0:T(8,128)(2,1)} %copy-done.1) | copy-start | bytes 3145732
  181.3 48.7 %reduce-scatter.9.cloned.1.call-start = ((), (), s32[]{:S(2)}) async-start(), calls=%async_computation.9 | async-start | bytes 1474560 | tf_op jit(solution)/shard_map/reduce_scatter | solution.py:22
  194.6 97.5 %reduce-scatter.11.cloned.1.call-start = ((), (), s32[]{:S(2)}) async-start(), calls=%async_computation.10 | async-start | bytes 319488 | tf_op jit(solution)/shard_map/reduce_scatter | solution.py:22
Sparse Core Ops, SparseCore 0:
  12.5 122.2 all-gather.1
  181.4 13.1 reduce-scatter.6
  197.7 32.2 reduce-scatter.8
  233.6 58.4 reduce-scatter.10
Sparse Core Ops, SparseCore 1:
  18.3 106.6 reduce-scatter.4
where the time goes:
time: 300 us; the launch traced here: 299 us
  waiting for transfers between devices  239 us (80%)
  between operations  15.4 us (5%)
  blocking collectives  14.1 us (5%)
  matrix products  11.6 us (4%)
  local copies, waits for them, and re-layouts  9.17 us (3%)
  starting transfers between devices  6.94 us (2%)
    all_gather x1, waiting for transfers between devices, body(): gathered = lax.all_gather(proj_flat, DP, axis=0, tiled=True)  117 us
    reduce_scatter x3, waiting for transfers between devices, own_block(): blocks = lax.psum_scatter(blocks, axes[k], scatter_dimension=0, tiled=True)  110 us
    all_to_all x1, blocking collectives, body(): lax.all_to_all(image_own, 'mp', split_axis=1, concat_axis=0, tiled=True)  14.1 us
    all_to_all x1, waiting for transfers between devices, body(): lax.all_to_all(embed_cols, 'mp', split_axis=0, concat_axis=1, tiled=True)  12 us
    dot_general x1, matrix products, row_term(): lax.dot_general(left, weight, (((1,), (1,)), ((), ())), preferred_element...  8.93 us
    all_to_all x1, starting transfers between devices, body(): lax.all_to_all(embed_cols, 'mp', split_axis=0, concat_axis=1, tiled=True)  6.74 us
  transfers between devices with their start and end apart: 6, of which 5 were waited for; matrix products, arithmetic and copies ran while one was open for 4% of the time, Pallas kernels for 0%

commit v1 on v0

v1 whole, which is shorter than its diff:
```python
import functools

import jax
import jax.numpy as jnp
from jax import lax
from jax.experimental import pallas as pl
from jax.experimental.pallas import tpu as pltpu
from jax.sharding import Mesh
from jax.sharding import PartitionSpec as P

IMG_MAX = 4
PATCH = 8
IMG = IMG_MAX * PATCH
LANES = 128
DP = ("dp_0", "dp_1", "dp_2")
DP_MP = ("dp_0", "dp_1", "dp_2", "mp")
EPS = 1e-05
MESH = pl.DeviceIdType.MESH
F32 = jnp.float32
BF16 = jnp.bfloat16


def dot_nt(a, b):
    return lax.dot_general(a, b, (((1,), (1,)), ((), ())), preferred_element_type=F32)


def dot_tn(a, b):
    return lax.dot_general(a, b, (((0,), (0,)), ((), ())), preferred_element_type=F32)


def kernel(
    sizes,
    vis_h,
    count_s,
    proj_h,
    text_h,
    gain_h,
    qw_h,
    qg_h,
    text_o,
    proj_o,
    qw,
    qi,
    qt,
    vis,
    txt,
    gain,
    ag,
    flat,
    wblk,
    ib,
    tb,
    gtxt,
    part,
    st,
    st_in,
    hs,
    hc,
    h1,
    hx,
    h2,
    hz,
    stage_t,
    stage_p,
    load_sem,
    out_sem,
    agz_s,
    agz_r,
    agx_s,
    agx_r,
    agc_s,
    agc_r,
    is_s,
    is_r,
    ts_s,
    ts_r,
    st_s,
    st_r,
    rc_s,
    rc_r,
    rx_s,
    rx_r,
    rz_s,
    rz_r,
):
    nz, nx, ny = sizes
    z = lax.axis_index("dp_0")
    x = lax.axis_index("dp_1")
    c = lax.axis_index("dp_2")
    y = lax.axis_index("mp")
    width = qw.shape[1]
    total = qw.shape[0]
    enc = vis.shape[1]
    text_rows = txt.shape[0]
    img_all = qi.shape[0]
    img_half = img_all // 2
    near = ny // 2
    slices = tb.shape[2]
    in_half = slices // 2
    tw = tb.shape[4]
    packed = width // LANES
    shard = proj_h.shape[0]
    live_shards = -(-enc * packed // shard)
    other = 1 - c

    def ring(i, n):
        return lax.rem(i, n)

    barrier = pltpu.get_barrier_semaphore()

    def greet(axis, me, n):
        def one(j, carry):
            pl.semaphore_signal(
                barrier, inc=1, device_id={axis: ring(me + j, n)}, device_id_type=MESH
            )
            return carry

        lax.fori_loop(1, n, one, 0)

    greet("mp", y, ny)
    greet("dp_1", x, nx)
    greet("dp_0", z, nz)
    pl.semaphore_signal(barrier, inc=1, device_id={"dp_2": other}, device_id_type=MESH)

    def load(src, dst, i):
        return pltpu.make_async_copy(src, dst, load_sem.at[i])

    rows_each = IMG + text_rows
    load(proj_h, ag.at[c, x, z], 0).start()
    load(qw_h, qw, 1).start()

    def rows_in(k):
        base = pl.multiple_of(k * rows_each, 16)
        to_i = qi.at[pl.ds(pl.multiple_of(k * IMG, 16), IMG)]
        return (
            load(qg_h.at[pl.ds(base, IMG)], to_i, 6 + k),
            load(
                qg_h.at[pl.ds(pl.multiple_of(base + IMG, 16), text_rows)],
                qt.at[k],
                6 + ny + k,
            ),
        )

    def start_rows(k, carry):
        a, b = rows_in(k)
        a.start()
        b.start()
        return carry

    lax.fori_loop(0, ny, start_rows, 0)
    load(vis_h, vis, 2).start()
    load(text_h, txt, 3).start()
    load(gain_h, gain, 4).start()

    def wait_rows(k, carry):
        a, b = rows_in(k)
        a.wait()
        b.wait()
        return carry

    lax.fori_loop(0, ny, wait_rows, 0)
    load(qw_h, qw, 1).wait()

    def owner_of(way, d):
        return ring(y + d, ny) if way == 0 else ring(y + ny - d, ny)

    def toward(way):
        return ring(y + 1, ny) if way == 0 else ring(y + ny - 1, ny)

    def img_dot(owner, h):
        rows = qi[pl.ds(pl.multiple_of(h * img_half, 16), img_half), :]
        block = qw[pl.ds(pl.multiple_of(owner * width, width), width), :]
        return dot_nt(rows, block)

    def img_send(way, d, h):
        return pltpu.make_async_remote_copy(
            src_ref=ib.at[way, d, h],
            dst_ref=ib.at[way, d - 1, h],
            send_sem=is_s.at[way, d - 1, h],
            recv_sem=is_r.at[way, d - 1, h],
            device_id={"mp": toward(way)},
            device_id_type=MESH,
        )

    def img_first(way, far):
        d = near if far else near - 1
        h = way if far else 1 - way
        ib[way, d, h] = img_dot(owner_of(way, d), h).astype(BF16)

    def img_first_send(way, far):
        d = near if far else near - 1
        h = way if far else 1 - way
        img_send(way, d, h).start()

    def relay_place(u, way):
        d = near - 1 - (u + 1) // 2
        h = lax.rem(u, 2) if way == 0 else 1 - lax.rem(u, 2)
        return d, h

    def img_relay(u, carry):
        for way in (0, 1):
            d, h = relay_place(u, way)
            mine = img_dot(owner_of(way, d), h)
            img_send(way, d + 1, h).wait_recv()
            ib[way, d, h] = (mine + ib[way, d, h].astype(F32)).astype(BF16)
            img_send(way, d, h).start()
        return carry

    for way in (0, 1):
        img_first(way, True)
    for way in (0, 1):
        img_first(way, False)

    load(proj_h, ag.at[c, x, z], 0).wait()
    pl.semaphore_wait(barrier, (ny - 1) + (nx - 1) + (nz - 1) + 1)

    for way in (0, 1):
        img_first_send(way, True)

    def agz(j):
        return pltpu.make_async_remote_copy(
            src_ref=ag.at[c, x, z],
            dst_ref=ag.at[c, x, z],
            send_sem=agz_s,
            recv_sem=agz_r,
            device_id={"dp_0": ring(z + j, nz)},
            device_id_type=MESH,
        )

    def agx(j):
        return pltpu.make_async_remote_copy(
            src_ref=ag.at[c, x],
            dst_ref=ag.at[c, x],
            send_sem=agx_s,
            recv_sem=agx_r,
            device_id={"dp_1": ring(x + j, nx)},
            device_id_type=MESH,
        )

    agc = pltpu.make_async_remote_copy(
        src_ref=ag.at[c],
        dst_ref=ag.at[c],
        send_sem=agc_s,
        recv_sem=agc_r,
        device_id={"dp_2": other},
        device_id_type=MESH,
    )

    def begin(make, n):
        def one(j, carry):
            make(j).start()
            return carry

        lax.fori_loop(1, n, one, 0)

    def drain(ref, sem):
        pltpu.make_async_copy(ref, ref, sem).wait()

    begin(agz, nz)
    for way in (0, 1):
        img_first_send(way, False)

    relays = ny - 3
    early = min(2, relays)
    lax.fori_loop(0, early, img_relay, 0)
    drain(ag.at[0, 0, pl.ds(0, nz - 1)], agz_r)
    begin(agx, nx)
    lax.fori_loop(early, relays, img_relay, 0)

    def text_dot(owner, s):
        cols = qw[pl.ds(pl.multiple_of(s * tw, tw), tw), :]
        return dot_nt(qt[owner], cols)

    def text_send(way, d, s):
        return pltpu.make_async_remote_copy(
            src_ref=tb.at[way, d, s],
            dst_ref=tb.at[way, d - 1, s],
            send_sem=ts_s.at[way, d - 1, s],
            recv_sem=ts_r.at[way, d - 1, s],
            device_id={"mp": toward(way)},
            device_id_type=MESH,
        )

    def text_first(i, carry):
        far = i < in_half
        k = lax.rem(i, in_half)
        d = jnp.where(far, near, near - 1)
        for way in (0, 1):
            h = jnp.where(far, way, 1 - way)
            s = h * in_half + k
            tb[way, d, s] = text_dot(owner_of(way, d), s).astype(BF16)
            text_send(way, d, s).start()
        return carry

    def text_relay(n, carry):
        u = n // in_half
        k = lax.rem(n, in_half)
        for way in (0, 1):
            d, h = relay_place(u, way)
            s = h * in_half + k
            mine = text_dot(owner_of(way, d), s)
            text_send(way, d + 1, s).wait_recv()
            tb[way, d, s] = (mine + tb[way, d, s].astype(F32)).astype(BF16)
            text_send(way, d, s).start()
        return carry

    lax.fori_loop(0, 2, text_first, 0)

    drain(ag.at[0, pl.ds(0, nx - 1)], agx_r)
    agc.start()

    own_sum = [img_dot(y, h) for h in (0, 1)]
    load(vis_h, vis, 2).wait()
    load(gain_h, gain, 4).wait()
    drain(ag.at[0], agc_r)

    def unpack(s, carry):
        zz, r = s // (2 * nx), lax.rem(s, 2 * nx)
        rows = pl.ds(pl.multiple_of(s * shard, 16), shard)
        flat[rows, :] = ag[lax.rem(r, 2), r // 2, zz].astype(F32)
        return carry

    lax.fori_loop(0, live_shards, unpack, 0)
    for q in range(packed):
        wblk[:, q * LANES : (q + 1) * LANES] = flat[pl.ds(q, enc, packed), :].astype(BF16)
    embed = jnp.dot(vis[...], wblk[...], preferred_element_type=F32).astype(BF16)
    embed = embed.astype(F32)

    sums = []
    for h in (0, 1):
        mine = own_sum[h]
        for way in (0, 1):
            img_send(way, 1, h).wait_recv()
            mine = mine + ib[way, 0, h].astype(F32)
        sums.append(mine)
    gain_block = gain[:, pl.ds(pl.multiple_of(y * width, LANES), width)]
    scaled = gain_block * jnp.concatenate(sums, axis=0)
    sq = jnp.sum(embed * embed, axis=1, keepdims=True)
    cross = jnp.sum(scaled * embed, axis=1, keepdims=True)
    lane = lax.broadcasted_iota(jnp.int32, (img_all, LANES), 1)
    both = jnp.where(lane == 0, sq, jnp.where(lane == 1, cross, 0.0))
    st[...] = both.T[:8, :]

    def st_send(j):
        return pltpu.make_async_remote_copy(
            src_ref=st,
            dst_ref=st_in.at[j - 1],
            send_sem=st_s,
            recv_sem=st_r,
            device_id={"mp": ring(y + j, ny)},
            device_id_type=MESH,
        )

    begin(st_send, ny)
    part[0:img_all, :] = scaled
    part[img_all : 2 * img_all, :] = embed
    lax.fori_loop(2, 2 * in_half, text_first, 0)

    drain(st_in, st_r)
    stats = st[...]
    for j in range(ny - 1):
        stats = stats + st_in[j]
    stats = jnp.concatenate([stats, jnp.zeros((LANES - 8, img_all), F32)], axis=0).T
    inv = lax.rsqrt(stats[:, 0:1] * (1.0 / total) + EPS)
    mean = stats[:, 1:2] * (1.0 / total)
    row = lax.broadcasted_iota(jnp.int32, (img_all, 1), 0)
    counts = jnp.zeros((img_all, 1), jnp.int32)
    for k in range(ny):
        counts = jnp.where(row // IMG == k, count_s[k], counts)
    live = lax.rem(row, IMG) // PATCH < counts
    grad = inv * part[0:img_all, :] - part[img_all : 2 * img_all, :] * (inv * inv * inv * mean)
    grad = jnp.where(live, grad, 0.0).astype(BF16)

    for q in range(packed):
        cols = dot_tn(vis[...], grad[:, q * LANES : (q + 1) * LANES])
        flat[pl.ds(q, enc, packed), :] = cols
    pad = flat.shape[0] - enc * packed
    if pad:
        flat[enc * packed :, :] = jnp.zeros((pad, LANES), F32)

    def pack(s, carry):
        zz, r = s // (2 * nx), lax.rem(s, 2 * nx)
        rows = pl.ds(pl.multiple_of(s * shard, 16), shard)
        hs[lax.rem(r, 2), r // 2, zz] = flat[rows, :].astype(BF16)
        return carry

    lax.fori_loop(0, 2 * nx * nz, pack, 0)
    rc = pltpu.make_async_remote_copy(
        src_ref=hs.at[other],
        dst_ref=hc,
        send_sem=rc_s,
        recv_sem=rc_r,
        device_id={"dp_2": other},
        device_id_type=MESH,
    )
    rc.start()

    def rx(j):
        return pltpu.make_async_remote_copy(
            src_ref=h1.at[ring(x + j, nx)],
            dst_ref=hx.at[j - 1],
            send_sem=rx_s,
            recv_sem=rx_r,
            device_id={"dp_1": ring(x + j, nx)},
            device_id_type=MESH,
        )

    def rz(j):
        return pltpu.make_async_remote_copy(
            src_ref=h2.at[ring(z + j, nz)],
            dst_ref=hz.at[j - 1],
            send_sem=rz_s,
            recv_sem=rz_r,
            device_id={"dp_0": ring(z + j, nz)},
            device_id_type=MESH,
        )

    steps = relays * in_half
    cut = [min(k, steps) for k in (2, 8, 14)]
    lax.fori_loop(0, cut[0], text_relay, 0)

    rc.wait_recv()

    def core_sum(s, carry):
        xx, zz = s // nz, lax.rem(s, nz)
        h1[xx, zz] = (hs[c, xx, zz].astype(F32) + hc[xx, zz].astype(F32)).astype(BF16)
        return carry

    lax.fori_loop(0, nx * nz, core_sum, 0)
    begin(rx, nx)
    lax.fori_loop(cut[0], cut[1], text_relay, 0)

    drain(hx, rx_r)

    def x_sum(zz, carry):
        acc = h1[x, zz].astype(F32)
        for j in range(nx - 1):
            acc = acc + hx[j, zz].astype(F32)
        h2[zz] = acc.astype(BF16)
        return carry

    lax.fori_loop(0, nz, x_sum, 0)
    begin(rz, nz)

    load(text_h, txt, 3).wait()
    sq_t = jnp.zeros((text_rows, 1), F32)
    for s in range(slices):
        rows_t = txt[:, s * tw : (s + 1) * tw].astype(F32)
        sq_t = sq_t + jnp.sum(rows_t * rows_t, axis=1, keepdims=True)
    lax.fori_loop(cut[1], cut[2], text_relay, 0)

    drain(hz, rz_r)
    acc = h2[z].astype(F32)
    for j in range(nz - 1):
        acc = acc + hz[j].astype(F32)
    stage_p[...] = acc * (float(nz * nx * 2 * img_all) ** -0.5)
    out_p = pltpu.make_async_copy(stage_p, proj_o, out_sem.at[0])
    out_p.start()
    lax.fori_loop(cut[2], steps, text_relay, 0)

    cross_t = jnp.zeros((text_rows, 1), F32)
    for k in range(in_half):
        for h in (1, 0):
            s = h * in_half + k
            g = text_dot(y, s)
            for way in (0, 1):
                text_send(way, 1, s).wait_recv()
                g = g + tb[way, 0, s].astype(F32)
            g = g * gain[:, s * tw : (s + 1) * tw]
            gtxt[s] = g
            rows_t = txt[:, s * tw : (s + 1) * tw].astype(F32)
            cross_t = cross_t + jnp.sum(g * rows_t, axis=1, keepdims=True)
    inv_t = lax.rsqrt(sq_t * (1.0 / total) + EPS)
    scale_t = inv_t * inv_t * inv_t * (cross_t * (1.0 / total))
    for s in range(slices):
        rows_t = txt[:, s * tw : (s + 1) * tw].astype(F32)
        stage_t[:, s * tw : (s + 1) * tw] = (inv_t * gtxt[s] - rows_t * scale_t).astype(BF16)
    out_t = pltpu.make_async_copy(stage_t, text_o, out_sem.at[1])
    out_t.start()

    drain(ag.at[0, 0, pl.ds(0, nz - 1)], agz_s)
    drain(ag.at[0, pl.ds(0, nx - 1)], agx_s)
    agc.wait_send()
    drain(st_in, st_s)
    rc.wait_send()
    drain(hx, rx_s)
    drain(hz, rz_s)
    for way in (0, 1):
        for d in range(1, near + 1):
            for h in (0, 1):
                if d < near or h == way:
                    img_send(way, d, h).wait_send()

                    def sent(k, carry, way=way, d=d, h=h):
                        text_send(way, d, h * in_half + k).wait_send()
                        return carry

                    lax.fori_loop(0, in_half, sent, 0)
    out_p.wait()
    out_t.wait()


def body(vision_rows, image_count, proj_flat, text_embeds, norm_gain, q_weight, q_grad):
    nz, nx, ny = (lax.axis_size(a) for a in ("dp_0", "dp_1", "mp"))
    total, width = q_weight.shape
    img_all, enc = vision_rows.shape
    text_rows = text_embeds.shape[0]
    shard = proj_flat.shape[0]
    near = ny // 2
    slices = 8
    tw = total // slices
    flat_rows = nz * nx * 2 * shard
    sem = pltpu.SemaphoreType.DMA
    any_space = pl.BlockSpec(memory_space=pl.ANY)
    scratch = [
        pltpu.VMEM((total, width), BF16),
        pltpu.VMEM((img_all, width), BF16),
        pltpu.VMEM((ny, text_rows, width), BF16),
        pltpu.VMEM((img_all, enc), BF16),
        pltpu.VMEM((text_rows, total), BF16),
        pltpu.VMEM((1, total), F32),
        pltpu.VMEM((2, nx, nz, shard, LANES), BF16),
        pltpu.VMEM((flat_rows, LANES), F32),
        pltpu.VMEM((enc, width), BF16),
        pltpu.VMEM((2, near + 1, 2, img_all // 2, width), BF16),
        pltpu.VMEM((2, near + 1, slices, text_rows, tw), BF16),
        pltpu.VMEM((slices, text_rows, tw), F32),
        pltpu.VMEM((2 * img_all, width), F32),
        pltpu.VMEM((8, img_all), F32),
        pltpu.VMEM((ny - 1, 8, img_all), F32),
        pltpu.VMEM((2, nx, nz, shard, LANES), BF16),
        pltpu.VMEM((nx, nz, shard, LANES), BF16),
        pltpu.VMEM((nx, nz, shard, LANES), BF16),
        pltpu.VMEM((nx - 1, nz, shard, LANES), BF16),
        pltpu.VMEM((nz, shard, LANES), BF16),
        pltpu.VMEM((nz - 1, shard, LANES), BF16),
        pltpu.VMEM((text_rows, total), BF16),
        pltpu.VMEM((shard, LANES), F32),
        sem((6 + 2 * ny,)),
        sem((2,)),
        *([sem] * 6),
        sem((2, near, 2)),
        sem((2, near, 2)),
        sem((2, near, slices)),
        sem((2, near, slices)),
        *([sem] * 8),
    ]
    return pl.pallas_call(
        functools.partial(kernel, (nz, nx, ny)),
        out_shape=(
            jax.ShapeDtypeStruct(text_embeds.shape, BF16),
            jax.ShapeDtypeStruct(proj_flat.shape, F32),
        ),
        in_specs=[
            any_space,
            pl.BlockSpec(memory_space=pltpu.SMEM),
            *([any_space] * 5),
        ],
        out_specs=(any_space, any_space),
        scratch_shapes=scratch,
        compiler_params=pltpu.CompilerParams(
            collective_id=0,
            has_side_effects=True,
            vmem_limit_bytes=56 * 1024 * 1024,
        ),
        name="step",
    )(vision_rows, image_count, proj_flat, text_embeds, norm_gain.reshape(1, -1), q_weight, q_grad)


def solution(mesh):
    finer = Mesh(mesh.devices.reshape(12, 4, 2, mesh.shape["mp"]), ("dp_0", "dp_1", "dp_2", "mp"))
    placed = (P(DP, None), P(DP), P(DP_MP, None), P(DP_MP, None), P(), P(None, "mp"), P(DP, "mp"))
    return jax.shard_map(
        body,
        mesh=finer,
        in_specs=placed,
        out_specs=(P(DP_MP, None), P(DP_MP, None)),
        check_vma=False,
    )
```

time: 300 us -> 109 us (0.36)
  the two profiles are of different devices: /device:TPU:2 before, /device:TPU:1 now
where the time goes in v1:
time: 109 us
  Pallas kernels  105 us (96%)
  local copies, waits for them, and re-layouts  3.41 us (3%)
    pallas_call x1, Pallas kernels, body(): pl.pallas_call(functools.partial(kernel, (nz, nx, ny)), out_shape=(jax.Sh...  105 us
    unnamed x2, local copies, waits for them, and re-layouts  3.41 us

profile of v1, /device:TPU:1, one launch (start us, length us, event | category | flops | bytes accessed | tf_op | source)
XLA Modules:
  0.0 108.7 jit_solution(6341047805537484107)
XLA Ops:
  0.6 104.6 %step.1 = (bf16[96,4096]{1,0:T(8,128)(2,1)}, f32[48,128]{1,0:T(8,128)}) custom-call(bf16[256,1024]{1,0:T(8,128)(2,1)} %vis_h.1, s32[8]{0:T(128)} %count_s.1, bf16[48,128]{1,0:T(8,128)(2,1)} %proj_h.1, bf16[96,4096]{1,0:T(8,128)(2,1)} %text_h.1, f32[1,4096]{1,0:T(1,128)} %bitcast.1, bf16[4096,512]{1,0:T(8,128)(2,1)} %qw_h.1, bf16[1024,512]{1,0:T(8,128)(2,1)} %qg_h.1), custom_call_target="tpu_custom_call" | custom-call | tf_op jit(solution)/shard_map/step/pallas_call | solution.py:548
  105.3 2.1 %copy.11 = bf16[96,4096]{1,0:T(8,128)(2,1)} copy(bf16[96,4096]{1,0:T(8,128)(2,1)} %get-tuple-element.4) | data formatting | bytes 1572864
  107.3 1.3 %copy.12 = f32[48,128]{1,0:T(8,128)} copy(f32[48,128]{1,0:T(8,128)} %get-tuple-element.5) | data formatting | bytes 49152

commit v2 on v0

v2 whole, which is shorter than its diff:
```python
import functools

import jax
import jax.numpy as jnp
from jax import lax
from jax.experimental import pallas as pl
from jax.experimental.pallas import tpu as pltpu
from jax.sharding import Mesh
from jax.sharding import PartitionSpec as P

IMG_MAX = 4
PATCH = 8
IMG = IMG_MAX * PATCH
LANES = 128
DP = ("dp_0", "dp_1", "dp_2")
DP_MP = ("dp_0", "dp_1", "dp_2", "mp")
EPS = 1e-05
MESH = pl.DeviceIdType.MESH
F32 = jnp.float32
BF16 = jnp.bfloat16


def dot_nt(a, b):
    return lax.dot_general(a, b, (((1,), (1,)), ((), ())), preferred_element_type=F32)


def kernel(
    sizes,
    vis_h,
    count_s,
    proj_h,
    text_h,
    gain_h,
    qw_h,
    qg_h,
    text_o,
    proj_o,
    qw,
    qi,
    qt,
    vis,
    vis_t,
    txt,
    gain,
    sy,
    rows_f,
    lhs,
    ag,
    flat,
    wblk,
    emb,
    tb,
    gtxt,
    st,
    st_in,
    hs,
    hc,
    h1,
    hx,
    h2,
    hz,
    ty,
    ty_in,
    load_sem,
    sy_s,
    sy_r,
    agz_s,
    agz_r,
    agx_s,
    agx_r,
    agc_s,
    agc_r,
    ts_s,
    ts_r,
    st_s,
    st_r,
    rc_s,
    rc_r,
    rx_s,
    rx_r,
    rz_s,
    rz_r,
    ty_s,
    ty_r,
):
    nz, nx, ny = sizes
    z = lax.axis_index("dp_0")
    x = lax.axis_index("dp_1")
    c = lax.axis_index("dp_2")
    y = lax.axis_index("mp")
    total, width = qw.shape
    enc = vis.shape[1]
    text_rows = txt.shape[0]
    img_all = qi.shape[0]
    near = ny // 2
    slices = tb.shape[2]
    in_half = slices // 2
    tw = tb.shape[4]
    packed = width // LANES
    shard = proj_h.shape[0]
    own_rows = lhs.shape[0]
    live_shards = -(-enc * packed // shard)
    other = 1 - c
    per_row = 1.0 / total

    def ring(i, n):
        return lax.rem(i, n)

    def drain(ref, sem):
        pltpu.make_async_copy(ref, ref, sem).wait()

    def begin(make, n):
        def one(j, carry):
            make(j).start()
            return carry

        lax.fori_loop(1, n, one, 0)

    def send(src, dst, send_sem, recv_sem, axis, index):
        return pltpu.make_async_remote_copy(
            src_ref=src,
            dst_ref=dst,
            send_sem=send_sem,
            recv_sem=recv_sem,
            device_id={axis: index},
            device_id_type=MESH,
        )

    barrier = pltpu.get_barrier_semaphore()

    def greet(axis, me, n):
        def one(j, carry):
            pl.semaphore_signal(
                barrier, inc=1, device_id={axis: ring(me + j, n)}, device_id_type=MESH
            )
            return carry

        lax.fori_loop(1, n, one, 0)

    greet("dp_0", z, nz)
    greet("mp", y, ny)
    greet("dp_1", x, nx)
    pl.semaphore_signal(barrier, inc=1, device_id={"dp_2": other}, device_id_type=MESH)

    def load(src, dst, i):
        return pltpu.make_async_copy(src, dst, load_sem.at[i])

    rows_each = IMG + text_rows

    def text_in(k):
        base = pl.multiple_of(k * rows_each + IMG, 16)
        return load(qg_h.at[pl.ds(base, text_rows)], qt.at[k], 6 + k)

    def img_in(k):
        base = pl.multiple_of(k * rows_each, 16)
        to = qi.at[pl.ds(pl.multiple_of(k * IMG, 16), IMG)]
        return load(qg_h.at[pl.ds(base, IMG)], to, 6 + ny + k)

    def start_all(make):
        def one(k, carry):
            make(k).start()
            return carry

        lax.fori_loop(0, ny, one, 0)

    def wait_all(make):
        def one(k, carry):
            make(k).wait()
            return carry

        lax.fori_loop(0, ny, one, 0)

    load(proj_h, ag.at[0, c, x, z], 0).start()
    load(proj_h, sy.at[y], 5).start()
    start_all(text_in)
    load(qw_h, qw, 1).start()
    load(gain_h, gain, 4).start()
    load(vis_h, vis, 2).start()
    start_all(img_in)
    load(text_h, txt, 3).start()
    rows_f[...] = jnp.zeros(rows_f.shape, F32)
    wait_all(text_in)
    load(qw_h, qw, 1).wait()

    def owner_of(way, d):
        return ring(y + d, ny) if way == 0 else ring(y + ny - d, ny)

    def text_dot(owner, s):
        cols = qw[pl.ds(pl.multiple_of(s * tw, tw), tw), :]
        return dot_nt(qt[owner], cols)

    def text_send(way, d, s):
        return send(
            tb.at[way, d, s],
            tb.at[way, d - 1, s],
            ts_s.at[way, d - 1, s],
            ts_r.at[way, d - 1, s],
            "mp",
            ring(y + 1, ny) if way == 0 else ring(y + ny - 1, ny),
        )

    def first_place(i, way):
        far = i < in_half
        h = jnp.where(far, way, 1 - way)
        return jnp.where(far, near, near - 1), h * in_half + lax.rem(i, in_half)

    def text_first(i, carry):
        for way in (0, 1):
            d, s = first_place(i, way)
            tb[way, d, s] = text_dot(owner_of(way, d), s).astype(BF16)
            text_send(way, d, s).start()
        return carry

    def relay_place(n, way):
        u = n // in_half
        h = lax.rem(u, 2) if way == 0 else 1 - lax.rem(u, 2)
        return near - 1 - (u + 1) // 2, h * in_half + lax.rem(n, in_half)

    def text_relay(n, carry):
        for way in (0, 1):
            d, s = relay_place(n, way)
            mine = text_dot(owner_of(way, d), s)
            text_send(way, d + 1, s).wait_recv()
            tb[way, d, s] = (mine + tb[way, d, s].astype(F32)).astype(BF16)
            text_send(way, d, s).start()
        return carry

    steps = (ny - 3) * in_half
    firsts = 2 * in_half
    done = [0, 0]

    def first(n):
        upto = min(done[0] + n, firsts)
        lax.fori_loop(done[0], upto, text_first, 0)
        done[0] = upto

    def relay(n):
        upto = min(done[1] + n, steps)
        lax.fori_loop(done[1], upto, text_relay, 0)
        done[1] = upto

    def agz(k):
        ref = ag.at[k, c, x, z]
        return lambda j: send(ref, ref, agz_s.at[k], agz_r.at[k], "dp_0", ring(z + j, nz))

    def agx(k):
        ref = ag.at[k, c, x]
        return lambda j: send(ref, ref, agx_s.at[k], agx_r.at[k], "dp_1", ring(x + j, nx))

    def agc(k):
        ref = ag.at[k, c]
        return send(ref, ref, agc_s.at[k], agc_r.at[k], "dp_2", other)

    def agz_wait(k, sem):
        drain(ag.at[0, 0, 0, pl.ds(0, nz - 1)], sem.at[k])

    def agx_wait(k, sem):
        drain(ag.at[0, 0, pl.ds(0, nx - 1)], sem.at[k])

    def agc_wait(k):
        drain(ag.at[0, 0], agc_r.at[k])

    def rc(k):
        return send(hs.at[k, other], hc.at[k], rc_s.at[k], rc_r.at[k], "dp_2", other)

    def rx(k):
        return lambda j: send(
            h1.at[k, ring(x + j, nx)],
            hx.at[k, j - 1],
            rx_s.at[k],
            rx_r.at[k],
            "dp_1",
            ring(x + j, nx),
        )

    def rz(k):
        return lambda j: send(
            h2.at[k, ring(z + j, nz)],
            hz.at[k, j - 1],
            rz_s.at[k],
            rz_r.at[k],
            "dp_0",
            ring(z + j, nz),
        )

    def st_send(k):
        return lambda j: send(
            st.at[k], st_in.at[k, j - 1], st_s.at[k], st_r.at[k], "mp", ring(y + j, ny)
        )

    def sy_send(j):
        return send(sy.at[y], sy.at[y], sy_s, sy_r, "mp", ring(y + j, ny))

    def ty_send(j):
        to = ring(y + j, ny)
        return send(ty.at[to], ty_in.at[j - 1], ty_s, ty_r, "mp", to)

    def unpack(k):
        def one(s, carry):
            zz, r = s // (2 * nx), lax.rem(s, 2 * nx)
            rows = pl.ds(pl.multiple_of(s * shard, 16), shard)
            flat[rows, :] = ag[k, lax.rem(r, 2), r // 2, zz].astype(F32)
            return carry

        lax.fori_loop(0, live_shards, one, 0)
        for q in range(packed):
            wblk[:, q * LANES : (q + 1) * LANES] = flat[pl.ds(q, enc, packed), :].astype(BF16)

    def pack(k, block):
        for q in range(packed):
            flat[pl.ds(q, enc, packed), :] = block[:, q * LANES : (q + 1) * LANES]
        pad = flat.shape[0] - enc * packed
        if pad:
            flat[enc * packed :, :] = jnp.zeros((pad, LANES), F32)

        def one(s, carry):
            zz, r = s // (2 * nx), lax.rem(s, 2 * nx)
            rows = pl.ds(pl.multiple_of(s * shard, 16), shard)
            hs[k, lax.rem(r, 2), r // 2, zz] = flat[rows, :].astype(BF16)
            return carry

        lax.fori_loop(0, 2 * nx * nz, one, 0)

    def core_sum(k):
        rc(k).wait_recv()

        def one(s, carry):
            xx, zz = s // nz, lax.rem(s, nz)
            pair = hs[k, c, xx, zz].astype(F32) + hc[k, xx, zz].astype(F32)
            h1[k, xx, zz] = pair.astype(BF16)
            return carry

        lax.fori_loop(0, nx * nz, one, 0)

    def x_sum(k):
        drain(hx.at[k], rx_r.at[k])

        def one(zz, carry):
            acc = h1[k, x, zz].astype(F32)
            for j in range(nx - 1):
                acc = acc + hx[k, j, zz].astype(F32)
            h2[k, zz] = acc.astype(BF16)
            return carry

        lax.fori_loop(0, nz, one, 0)

    def z_sum(k):
        drain(hz.at[k], rz_r.at[k])
        acc = h2[k, z].astype(F32)
        for j in range(nz - 1):
            acc = acc + hz[k, j].astype(F32)
        return acc

    def publish(k, column):
        wide = jnp.broadcast_to(column, (img_all, LANES))
        st[k] = wide.T[0:1, :]
        begin(st_send(k), ny)

    def collected(k):
        drain(st_in.at[k], st_r.at[k])
        row = st[k]
        for j in range(ny - 1):
            row = row + st_in[k, j]
        return jnp.broadcast_to(row, (LANES, img_all)).T[:, 0:1]

    for way in (0, 1):
        d, s = first_place(0, way)
        tb[way, d, s] = text_dot(owner_of(way, d), s).astype(BF16)
    done[0] = 1
    load(proj_h, ag.at[0, c, x, z], 0).wait()
    load(proj_h, sy.at[y], 5).wait()
    pl.semaphore_wait(barrier, (ny - 1) + (nx - 1) + (nz - 1) + 1)

    begin(sy_send, ny)
    begin(agz(0), nz)
    for way in (0, 1):
        d, s = first_place(0, way)
        text_send(way, d, s).start()
    first(2)

    load(gain_h, gain, 4).wait()
    drain(sy.at[pl.ds(0, ny - 1)], sy_r)
    for m in range(ny):
        rows_f[m, 0:shard, :] = sy[m].astype(F32)
        for q in range(packed):
            cols = slice(m * width + q * LANES, m * width + (q + 1) * LANES)
            piece = rows_f[m, pl.ds(q, own_rows, packed), :] * gain[:, cols]
            lhs[:, cols] = piece.astype(BF16)
    prod = jnp.dot(lhs[...], qw[...], preferred_element_type=F32)
    for q in range(packed):
        rows_f[0, pl.ds(q, own_rows, packed), :] = prod[:, q * LANES : (q + 1) * LANES]
    ag[1, c, x, z] = rows_f[0, 0:shard, :].astype(BF16)
    begin(agz(1), nz)

    first(1)
    load(vis_h, vis, 2).wait()
    vis_t[...] = vis[...].T
    agz_wait(0, agz_r)
    begin(agx(0), nx)
    first(firsts)
    relay(1)
    agz_wait(1, agz_r)
    begin(agx(1), nx)
    relay(1)
    agx_wait(0, agx_r)
    agc(0).start()
    relay(2)

    wait_all(img_in)
    agc_wait(0)
    unpack(0)
    embed = jnp.dot(vis[...], wblk[...], preferred_element_type=F32).astype(BF16)
    emb[...] = embed
    embed = embed.astype(F32)
    publish(0, jnp.sum(embed * embed, axis=1, keepdims=True))
    agx_wait(1, agx_r)
    agc(1).start()
    relay(2)

    row = lax.broadcasted_iota(jnp.int32, (img_all, 1), 0)
    counts = jnp.zeros((img_all, 1), jnp.int32)
    for k in range(ny):
        counts = jnp.where(row // IMG == k, count_s[k], counts)
    live = lax.rem(row, IMG) // PATCH < counts
    inv = lax.rsqrt(collected(0) * per_row + EPS)
    left = jnp.where(live, inv * qi[...].astype(F32), 0.0).astype(BF16)
    pack(0, jnp.dot(vis_t[...], left, preferred_element_type=F32))
    rc(0).start()

    agc_wait(1)
    unpack(1)
    back = jnp.dot(vis[...], wblk[...], preferred_element_type=F32)
    publish(1, jnp.sum(back * qi[...].astype(F32), axis=1, keepdims=True))
    relay(1)
    core_sum(0)
    begin(rx(0), nx)
    relay(1)
    mean = collected(1) * per_row
    right = jnp.where(live, (inv * inv * inv * mean) * emb[...].astype(F32), 0.0).astype(BF16)
    pack(1, jnp.dot(vis_t[...], right, preferred_element_type=F32))
    rc(1).start()
    relay(2)
    x_sum(0)
    begin(rz(0), nz)
    relay(1)
    core_sum(1)
    begin(rx(1), nx)

    load(text_h, txt, 3).wait()
    sq_t = jnp.zeros((text_rows, 1), F32)
    for s in range(slices):
        rows_t = txt[:, s * tw : (s + 1) * tw].astype(F32)
        sq_t = sq_t + jnp.sum(rows_t * rows_t, axis=1, keepdims=True)
    relay(3)
    x_sum(1)
    begin(rz(1), nz)
    relay(2)

    rows_f[0, 0:shard, :] = z_sum(0)
    for q in range(packed):
        lhs[:, q * LANES : (q + 1) * LANES] = rows_f[0, pl.ds(q, own_rows, packed), :].astype(BF16)
    term = lhs[:, 0:width]
    for m in range(ny):
        out = dot_nt(term, qw[m * width : (m + 1) * width, :])
        for q in range(packed):
            rows_f[m, pl.ds(q, own_rows, packed), :] = out[:, q * LANES : (q + 1) * LANES]
        ty[m] = rows_f[m, 0:shard, :].astype(BF16)
    begin(ty_send, ny)
    relay(steps)

    for k in range(in_half):
        for h in (0, 1):
            s = h * in_half + k
            g = text_dot(y, s)
            text_send(1 - h, 1, s).wait_recv()
            gtxt[s] = g + tb[1 - h, 0, s].astype(F32)

    second = z_sum(1)
    drain(ty_in, ty_r)
    one_term = ty[y].astype(F32)
    for j in range(ny - 1):
        one_term = one_term + ty_in[j].astype(F32)
    at = lax.rem(lax.broadcasted_iota(jnp.int32, (shard, LANES), 0), packed)
    gain_own = jnp.zeros((shard, LANES), F32)
    for q in range(packed):
        cols = pl.ds(pl.multiple_of(y * width + q * LANES, LANES), LANES)
        gain_own = jnp.where(at == q, gain[:, cols], gain_own)
    proj_o[...] = (gain_own * one_term - second) * (float(nz * nx * 2 * img_all) ** -0.5)

    cross_t = jnp.zeros((text_rows, 1), F32)
    for k in range(in_half):
        for h in (0, 1):
            s = h * in_half + k
            text_send(h, 1, s).wait_recv()
            g = (gtxt[s] + tb[h, 0, s].astype(F32)) * gain[:, s * tw : (s + 1) * tw]
            gtxt[s] = g
            rows_t = txt[:, s * tw : (s + 1) * tw].astype(F32)
            cross_t = cross_t + jnp.sum(g * rows_t, axis=1, keepdims=True)
    inv_t = lax.rsqrt(sq_t * per_row + EPS)
    scale_t = inv_t * inv_t * inv_t * (cross_t * per_row)
    for s in range(slices):
        cols = slice(s * tw, (s + 1) * tw)
        text_o[:, cols] = (inv_t * gtxt[s] - txt[:, cols].astype(F32) * scale_t).astype(BF16)

    drain(sy.at[pl.ds(0, ny - 1)], sy_s)
    for k in (0, 1):
        agz_wait(k, agz_s)
        agx_wait(k, agx_s)
        agc(k).wait_send()
        drain(st_in.at[k], st_s.at[k])
        rc(k).wait_send()
        drain(hx.at[k], rx_s.at[k])
        drain(hz.at[k], rz_s.at[k])
    drain(ty_in, ty_s)
    for way in (0, 1):
        for d in range(1, near + 1):
            for h in (0, 1):
                if d < near or h == way:

                    def sent(k, carry, way=way, d=d, h=h):
                        text_send(way, d, h * in_half + k).wait_send()
                        return carry

                    lax.fori_loop(0, in_half, sent, 0)


def put_out(text_v, proj_v, text_o, proj_o, sems):
    a = pltpu.make_async_copy(text_v, text_o, sems.at[0])
    b = pltpu.make_async_copy(proj_v, proj_o, sems.at[1])
    a.start()
    b.start()
    a.wait()
    b.wait()


def body(vision_rows, image_count, proj_flat, text_embeds, norm_gain, q_weight, q_grad):
    nz, nx, ny = (lax.axis_size(a) for a in ("dp_0", "dp_1", "mp"))
    total, width = q_weight.shape
    img_all, enc = vision_rows.shape
    text_rows = text_embeds.shape[0]
    shard = proj_flat.shape[0]
    packed = width // LANES
    own_rows = -(-shard // packed // 16) * 16
    near = ny // 2
    slices = 8
    tw = total // slices
    flat_rows = nz * nx * 2 * shard
    sem = pltpu.SemaphoreType.DMA
    any_space = pl.BlockSpec(memory_space=pl.ANY)
    in_vmem = pl.BlockSpec(memory_space=pltpu.VMEM)
    scratch = [
        pltpu.VMEM((total, width), BF16),
        pltpu.VMEM((img_all, width), BF16),
        pltpu.VMEM((ny, text_rows, width), BF16),
        pltpu.VMEM((img_all, enc), BF16),
        pltpu.VMEM((enc, img_all), BF16),
        pltpu.VMEM((text_rows, total), BF16),
        pltpu.VMEM((1, total), F32),
        pltpu.VMEM((ny, shard, LANES), BF16),
        pltpu.VMEM((ny, own_rows * packed, LANES), F32),
        pltpu.VMEM((own_rows, total), BF16),
        pltpu.VMEM((2, 2, nx, nz, shard, LANES), BF16),
        pltpu.VMEM((flat_rows, LANES), F32),
        pltpu.VMEM((enc, width), BF16),
        pltpu.VMEM((img_all, width), BF16),
        pltpu.VMEM((2, near + 1, slices, text_rows, tw), BF16),
        pltpu.VMEM((slices, text_rows, tw), F32),
        pltpu.VMEM((2, 1, img_all), F32),
        pltpu.VMEM((2, ny - 1, 1, img_all), F32),
        pltpu.VMEM((2, 2, nx, nz, shard, LANES), BF16),
        pltpu.VMEM((2, nx, nz, shard, LANES), BF16),
        pltpu.VMEM((2, nx, nz, shard, LANES), BF16),
        pltpu.VMEM((2, nx - 1, nz, shard, LANES), BF16),
        pltpu.VMEM((2, nz, shard, LANES), BF16),
        pltpu.VMEM((2, nz - 1, shard, LANES), BF16),
        pltpu.VMEM((ny, shard, LANES), BF16),
        pltpu.VMEM((ny - 1, shard, LANES), BF16),
        sem((6 + 2 * ny,)),
        sem,
        sem,
        *([sem((2,))] * 6),
        sem((2, near, slices)),
        sem((2, near, slices)),
        *([sem((2,))] * 8),
        sem,
        sem,
    ]
    text_v, proj_v = pl.pallas_call(
        functools.partial(kernel, (nz, nx, ny)),
        out_shape=(pltpu.VMEM(text_embeds.shape, BF16), pltpu.VMEM(proj_flat.shape, F32)),
        in_specs=[
            any_space,
            pl.BlockSpec(memory_space=pltpu.SMEM),
            *([any_space] * 5),
        ],
        out_specs=(in_vmem, in_vmem),
        scratch_shapes=scratch,
        compiler_params=pltpu.CompilerParams(
            collective_id=0,
            has_side_effects=True,
            vmem_limit_bytes=56 * 1024 * 1024,
        ),
        name="step",
    )(vision_rows, image_count, proj_flat, text_embeds, norm_gain.reshape(1, -1), q_weight, q_grad)
    return pl.pallas_call(
        put_out,
        out_shape=(
            jax.ShapeDtypeStruct(text_embeds.shape, BF16),
            jax.ShapeDtypeStruct(proj_flat.shape, F32),
        ),
        in_specs=[in_vmem] * 2,
        out_specs=(any_space, any_space),
        scratch_shapes=[sem((2,))],
        name="put_out",
    )(*(pltpu.with_memory_space_constraint(v, pltpu.VMEM) for v in (text_v, proj_v)))


def solution(mesh):
    finer = Mesh(mesh.devices.reshape(12, 4, 2, mesh.shape["mp"]), ("dp_0", "dp_1", "dp_2", "mp"))
    placed = (P(DP, None), P(DP), P(DP_MP, None), P(DP_MP, None), P(), P(None, "mp"), P(DP, "mp"))
    return jax.shard_map(
        body,
        mesh=finer,
        in_specs=placed,
        out_specs=(P(DP_MP, None), P(DP_MP, None)),
        check_vma=False,
    )
```

time: 300 us -> 94.3 us (0.31)
  the two profiles are of different devices: /device:TPU:2 before, /device:TPU:1 now
where the time goes in v2:
time: 94.3 us; the launch traced here: 93.1 us
  Pallas kernels  92.4 us (98%)
    pallas_call x1, Pallas kernels, body(): pl.pallas_call(functools.partial(kernel, (nz, nx, ny)), out_shape=(pltpu....  91.5 us

profile of v2, /device:TPU:1, one launch (start us, length us, event | category | flops | bytes accessed | tf_op | source)
XLA Modules:
  0.0 93.1 jit_solution(4592750917627886802)
XLA Ops:
  0.6 91.5 %step.1 = (bf16[96,4096]{1,0:T(8,128)(2,1)S(1)}, f32[48,128]{1,0:T(8,128)S(1)}) custom-call(bf16[256,1024]{1,0:T(8,128)(2,1)} %vis_h.1, s32[8]{0:T(128)} %count_s.1, bf16[48,128]{1,0:T(8,128)(2,1)} %proj_h.1, bf16[96,4096]{1,0:T(8,128)(2,1)} %text_h.1, f32[1,4096]{1,0:T(1,128)} %bitcast.1, bf16[4096,512]{1,0:T(8,128)(2,1)} %qw_h.1, bf16[1024,512]{1,0:T(8,128)(2,1)} %qg_h.1), custom_call_target="tpu_custom_call" | custom-call | tf_op jit(solution)/shard_map/step/pallas_call | solution.py:588
  92.2 0.9 put_out.1

commit v3 on v2

v3 whole, which is shorter than its diff:
```python
import functools

import jax
import jax.numpy as jnp
from jax import lax
from jax.experimental import pallas as pl
from jax.experimental.pallas import tpu as pltpu
from jax.sharding import Mesh
from jax.sharding import PartitionSpec as P

IMG_MAX = 4
PATCH = 8
IMG = IMG_MAX * PATCH
LANES = 128
DP = ("dp_0", "dp_1", "dp_2")
DP_MP = ("dp_0", "dp_1", "dp_2", "mp")
EPS = 1e-05
LEAD = 5
EARLY = 5
MESH = pl.DeviceIdType.MESH
F32 = jnp.float32
BF16 = jnp.bfloat16


def dot_nt(a, b):
    return lax.dot_general(a, b, (((1,), (1,)), ((), ())), preferred_element_type=F32)


def kernel(
    sizes,
    vis_h,
    count_h,
    proj_h,
    text_h,
    gain_h,
    qw_h,
    qg_h,
    text_o,
    proj_o,
    qw,
    qi,
    qt,
    vis,
    vis_t,
    txt,
    gain,
    sy,
    rows_f,
    lhs,
    ag,
    flat,
    wblk,
    emb,
    tb,
    gtxt,
    cross_f,
    st,
    st_in,
    hs,
    hc,
    h1,
    hx,
    h2,
    hz,
    ty,
    ty_in,
    count_s,
    in_sem,
    y_sem,
    load_sem,
    sy_s,
    sy_r,
    agz_s,
    agz_r,
    agx_s,
    agx_r,
    agc_s,
    agc_r,
    ts_s,
    ts_r,
    st_s,
    st_r,
    rc_s,
    rc_r,
    rx_s,
    rx_r,
    rz_s,
    rz_r,
    ty_s,
    ty_r,
):
    nz, nx, ny = sizes
    z = lax.axis_index("dp_0")
    x = lax.axis_index("dp_1")
    c = lax.axis_index("dp_2")
    y = lax.axis_index("mp")
    total, width = qw.shape
    enc = vis.shape[1]
    text_rows = txt.shape[0]
    img_all = qi.shape[0]
    near = ny // 2
    slices = gtxt.shape[0]
    in_half = slices // 2
    tw = tb.shape[3]
    packed = width // LANES
    shard = proj_h.shape[0]
    own_rows = lhs.shape[0]
    live_z = hx.shape[2]
    other = 1 - c
    per_row = 1.0 / total

    def ring(i, n):
        return lax.rem(i, n)

    def drain(ref, sem):
        pltpu.make_async_copy(ref, ref, sem).wait()

    def begin(make, n):
        def one(i, carry):
            side = jnp.where(lax.rem(i, 2) == 1, (i + 1) // 2, -(i // 2))
            make(n // 2 + side).start()
            return carry

        lax.fori_loop(0, n - 1, one, 0)

    def send(src, dst, send_sem, recv_sem, axis, index):
        return pltpu.make_async_remote_copy(
            src_ref=src,
            dst_ref=dst,
            send_sem=send_sem,
            recv_sem=recv_sem,
            device_id={axis: index},
            device_id_type=MESH,
        )

    def load(src, dst, i):
        return pltpu.make_async_copy(src, dst, load_sem.at[i])

    rows_each = IMG + text_rows

    def text_in(k, i):
        base = pl.multiple_of(k * rows_each + IMG, 16)
        return load(qg_h.at[pl.ds(base, text_rows)], qt.at[k], i)

    def img_in(k):
        base = pl.multiple_of(k * rows_each, 16)
        to = qi.at[pl.ds(pl.multiple_of(k * IMG, 16), IMG)]
        return load(qg_h.at[pl.ds(base, IMG)], to, 7)

    def slice_in(s):
        cols = pl.ds(pl.multiple_of(s * tw, tw), tw)
        return load(qw_h.at[cols], qw.at[cols], 9 + lax.rem(s, in_half))

    def pair_wait(i):
        drain(qw.at[pl.ds(0, 2 * tw)], load_sem.at[9 + i])

    def each(n, act, lo=0):
        def one(k, carry):
            act(k)
            return carry

        lax.fori_loop(lo, n, one, 0)

    load(proj_h, ag.at[0, c, x, z], 0).start()
    load(proj_h, sy.at[y], 1).start()
    text_in(ring(y + near, ny), 5).start()
    slice_in(0).start()
    slice_in(in_half).start()

    barrier = pltpu.get_barrier_semaphore()

    def tell(what, axis, index):
        pl.semaphore_signal(what, inc=1, device_id={axis: index}, device_id_type=MESH)

    corner_z = ((x == 0) & (y == 0) & (c == 0)).astype(jnp.int32)
    corner_x = ((z == 0) & (y == 0) & (c == 0)).astype(jnp.int32)
    corner_y = ((z == 0) & (x == 0) & (c == 0)).astype(jnp.int32)
    rank_z = ring(z + nz - corner_z, nz)
    rank_x = ring(x + nx - corner_x, nx)

    def tell_z(what):
        return lambda r: tell(what, "dp_0", ring(r + corner_z, nz))

    def tell_x(what):
        return lambda r: tell(what, "dp_1", ring(r + corner_x, nx))

    def turn(v):
        return ring(jnp.where(v < near, v, ny + near - 1 - v) + ny - corner_y, ny)

    def awaits(a, b, j):
        return (turn(b) < turn(a)) | (j == 1) | (j == ny - 1)

    y_now = jnp.int32(0)
    for j in range(1, ny):
        v = ring(y + j, ny)
        y_now = y_now + awaits(y, v, j).astype(jnp.int32)

        @pl.when(awaits(v, y, j))
        def _(v=v):
            tell(barrier, "mp", v)

    each(nz, tell_z(barrier), rank_z + 1)
    each(nx, tell_x(barrier), rank_x + 1)

    @pl.when(c == 1)
    def _():
        tell(barrier, "dp_2", other)

    def next_slices(i):
        slice_in(i).start()
        slice_in(in_half + i).start()

    each(in_half, next_slices, 1)
    each(ny, lambda j: text_in(ring(y + near + j, ny), 6).start(), 1)
    load(gain_h, gain, 4).start()
    load(vis_h, vis, 2).start()
    each(ny, lambda k: img_in(k).start())
    load(text_h, txt, 3).start()
    load(count_h, count_s, 8).start()

    def owner_of(way, d):
        return ring(y + d, ny) if way == 0 else ring(y + ny - d, ny)

    def text_dot(owner, s):
        cols = qw[pl.ds(pl.multiple_of(s * tw, tw), tw), :]
        return dot_nt(qt[owner], cols)

    mid_sems = (near - 1) * slices // 2

    def arrival(way, d, h, k):
        mid = ((d - 1) * slices + h * in_half + k) // 2
        end = mid_sems + jnp.where(h == way, 1 + k, 0)
        return ts_r.at[way, jnp.where(d > 0, mid, end)]

    def text_send(way, d, h, k):
        s = h * in_half + k
        return send(
            tb.at[way, d * slices + s],
            tb.at[way, (d - 1) * slices + s],
            ts_s.at[way],
            arrival(way, d - 1, h, k),
            "mp",
            ring(y + 1, ny) if way == 0 else ring(y + ny - 1, ny),
        )

    def text_first(i):
        far = i < in_half
        k = lax.rem(i, in_half)
        for way in (0, 1):
            h = jnp.where(far, way, 1 - way)
            d = jnp.where(far, near, near - 1)
            s = h * in_half + k
            tb[way, d * slices + s] = text_dot(owner_of(way, d), s).astype(BF16)
            text_send(way, d, h, k).start()

    def text_next_first(i):
        @pl.when(i < in_half)
        def _():
            pair_wait(i)

        text_first(i)

    def text_relay(n):
        u = n // in_half
        k = lax.rem(n, in_half)
        d = near - 1 - (u + 1) // 2
        for way in (0, 1):
            h = lax.rem(u + way, 2)
            s = h * in_half + k
            slot = d * slices + s
            mine = text_dot(owner_of(way, d), s)

            @pl.when(lax.rem(k, 2) == 0)
            def _(way=way, d=d, h=h, k=k):
                drain(tb.at[way, pl.ds(0, 2)], arrival(way, d, h, k))

            tb[way, slot] = (mine + tb[way, slot].astype(F32)).astype(BF16)
            text_send(way, d, h, k).start()

    steps = (ny - 3) * in_half
    firsts = 2 * in_half
    pieces = firsts + steps
    ahead = jnp.maximum(LEAD - 3 * z // 4, 0) + jnp.maximum((5 - turn(y)) // 2, 0)
    out = [jnp.int32(1), 1]

    def pace(n, most=None, times=1, more=0):
        most = min(n + LEAD + 2 if most is None else most, pieces)
        upto = jnp.minimum(n + times * ahead + more, most)
        upto = jnp.maximum(upto, out[0])
        if out[1] < firsts:
            each(jnp.minimum(upto, firsts), text_next_first, jnp.minimum(out[0], firsts))
        if most > firsts:
            each(jnp.maximum(upto, firsts) - firsts, text_relay, jnp.maximum(out[0], firsts) - firsts)
        out[0], out[1] = upto, max(out[1], min(n, pieces))

    def text_near(k):
        @pl.when(k == 0)
        def _():
            for way in (0, 1):
                drain(tb.at[way, pl.ds(0, in_half)], arrival(way, 0, 1 - way, 0))

        for h in (0, 1):
            s = h * in_half + k
            gtxt[s] = text_dot(y, s) + tb[1 - h, s].astype(F32)

    def text_last(k):
        for h in (0, 1):
            s = h * in_half + k
            drain(tb.at[h, 0], arrival(h, 0, h, k))
            cols = pl.ds(pl.multiple_of(s * tw, LANES), tw)
            g = (gtxt[s] + tb[h, s].astype(F32)) * gain[:, cols]
            gtxt[s] = g
            prod = g * txt[:, cols].astype(F32)
            for q in range(tw // LANES):
                cross_f[...] += prod[:, q * LANES : (q + 1) * LANES]

    def agz(k):
        ref = ag.at[k, c, x, z]
        return lambda j: send(ref, ref, agz_s.at[k], agz_r.at[k], "dp_0", ring(z + j, nz))

    def agx(k):
        ref = ag.at[k, c, x, pl.ds(0, live_z)]
        return lambda j: send(ref, ref, agx_s.at[k], agx_r.at[k], "dp_1", ring(x + j, nx))

    def agc(k):
        ref = ag.at[k, c]
        return send(ref, ref, agc_s.at[k], agc_r.at[k], "dp_2", other)

    def agz_wait(k, sem):
        drain(ag.at[0, 0, 0, pl.ds(0, nz - 1)], sem.at[k])

    def agx_wait(k, sem):
        drain(ag.at[0, 0, pl.ds(0, nx - 1), pl.ds(0, live_z)], sem.at[k])

    def agc_wait(k):
        drain(ag.at[0, 0], agc_r.at[k])

    def rc(k):
        live = pl.ds(0, live_z)
        return send(
            hs.at[k, other, :, live], hc.at[k, :, live], rc_s.at[k], rc_r.at[k], "dp_2", other
        )

    def rx(k):
        return lambda j: send(
            h1.at[k, ring(x + j, nx), pl.ds(0, live_z)],
            hx.at[k, j - 1],
            rx_s.at[k],
            rx_r.at[k],
            "dp_1",
            ring(x + j, nx),
        )

    def rz(k):
        return lambda j: send(
            h2.at[k, ring(z + j, nz)],
            hz.at[k, j - 1],
            rz_s.at[k],
            rz_r.at[k],
            "dp_0",
            ring(z + j, nz),
        )

    def st_send(k):
        return lambda j: send(
            st.at[k], st_in.at[k, j - 1], st_s.at[k], st_r.at[k], "mp", ring(y + j, ny)
        )

    def sy_send(j):
        return send(sy.at[y], sy.at[y], sy_s, sy_r, "mp", ring(y + j, ny))

    def ty_send(j):
        to = ring(y + j, ny)
        return send(ty.at[to], ty_in.at[j - 1], ty_s, ty_r, "mp", to)

    def place(zz, r):
        return pl.ds(pl.multiple_of((zz * 2 * nx + r) * shard, 16), shard)

    def unpack(k):
        def one(zz):
            for r in range(2 * nx):
                flat[place(zz, r), :] = ag[k, r % 2, r // 2, zz].astype(F32)

        each(live_z, one)
        for q in range(packed):
            wblk[:, q * LANES : (q + 1) * LANES] = flat[pl.ds(q, enc, packed), :].astype(BF16)

    def pack(k, block):
        for q in range(packed):
            flat[pl.ds(q, enc, packed), :] = block[:, q * LANES : (q + 1) * LANES]
        end = live_z * 2 * nx * shard
        if end > enc * packed:
            flat[enc * packed : end, :] = jnp.zeros((end - enc * packed, LANES), F32)

        def one(zz):
            for r in range(2 * nx):
                hs[k, r % 2, r // 2, zz] = flat[place(zz, r), :].astype(BF16)

        each(live_z, one)

    def core_sum(k):
        rc(k).wait_recv()

        def one(zz):
            for xx in range(nx):
                pair = hs[k, c, xx, zz].astype(F32) + hc[k, xx, zz].astype(F32)
                h1[k, xx, zz] = pair.astype(BF16)

        each(live_z, one)

    def x_sum(k):
        drain(hx.at[k], rx_r.at[k])

        def one(zz):
            acc = h1[k, x, zz].astype(F32)
            for j in range(nx - 1):
                acc = acc + hx[k, j, zz].astype(F32)
            h2[k, zz] = acc.astype(BF16)

        each(live_z, one)

    def z_sum(k):
        drain(hz.at[k], rz_r.at[k])
        acc = h2[k, z].astype(F32)
        for j in range(nz - 1):
            acc = acc + hz[k, j].astype(F32)
        return acc

    def publish(k, column):
        wide = jnp.broadcast_to(column, (img_all, LANES))
        st[k] = wide.T[0:1, :]
        begin(st_send(k), ny)

    def collected(k):
        drain(st_in.at[k], st_r.at[k])
        row = st[k]
        for j in range(ny - 1):
            row = row + st_in[k, j]
        return jnp.broadcast_to(row, (LANES, img_all)).T[:, 0:1]

    pl.semaphore_wait(barrier, y_now + rank_z + rank_x + other)
    each(rank_z, tell_z(in_sem))
    each(rank_x, tell_x(in_sem))

    @pl.when(c == 0)
    def _():
        tell(in_sem, "dp_2", other)

    for j in range(1, ny):
        v = ring(y + j, ny)

        @pl.when(jnp.logical_not(awaits(v, y, j)))
        def _(v=v):
            tell(y_sem, "mp", v)

    pair_wait(0)
    text_in(ring(y + near, ny), 5).wait()
    text_first(jnp.int32(0))
    load(proj_h, sy.at[y], 1).wait()
    load(proj_h, ag.at[0, c, x, z], 0).wait()
    drain(qt.at[pl.ds(0, ny - 1)], load_sem.at[6])

    early = z < EARLY
    pace(1, 3, 0, (ny - 1 - turn(y)) // 3)

    @pl.when(y_now < ny - 1)
    def _():
        pl.semaphore_wait(y_sem, ny - 1 - y_now)

    begin(sy_send, ny)
    pace(1, firsts + 2, 2)
    rest = (nz - 1 - rank_z) + (nx - 1 - rank_x) + c

    @pl.when(rest > 0)
    def _():
        pl.semaphore_wait(in_sem, rest)

    begin(agz(0), nz)
    rows_f[...] = jnp.zeros(rows_f.shape, F32)
    cross_f[...] = jnp.zeros(cross_f.shape, F32)
    for k in (0, 1):
        h2[k, live_z:] = jnp.zeros((nz - live_z, shard, LANES), BF16)
    pace(4)
    load(vis_h, vis, 2).wait()
    vis_t[...] = vis[...].T
    pace(6)
    agz_wait(0, agz_r)
    begin(agx(0), nx)

    load(gain_h, gain, 4).wait()
    drain(sy.at[pl.ds(0, ny - 1)], sy_r)
    for m in range(ny):
        rows_f[m, 0:shard, :] = sy[m].astype(F32)
        for q in range(packed):
            cols = slice(m * width + q * LANES, m * width + (q + 1) * LANES)
            piece = rows_f[m, pl.ds(q, own_rows, packed), :] * gain[:, cols]
            lhs[:, cols] = piece.astype(BF16)
    prod = jnp.dot(lhs[...], qw[...], preferred_element_type=F32)
    for q in range(packed):
        rows_f[0, pl.ds(q, own_rows, packed), :] = prod[:, q * LANES : (q + 1) * LANES]
    ag[1, c, x, z] = rows_f[0, 0:shard, :].astype(BF16)
    begin(agz(1), nz)
    pace(9)
    agx_wait(0, agx_r)
    agc(0).start()

    drain(qi, load_sem.at[7])
    agz_wait(1, agz_r)
    begin(agx(1), nx)
    agc_wait(0)
    unpack(0)
    embed = jnp.dot(vis[...], wblk[...], preferred_element_type=F32).astype(BF16)
    emb[...] = embed
    embed = embed.astype(F32)
    publish(0, jnp.sum(embed * embed, axis=1, keepdims=True))
    pace(12)

    agx_wait(1, agx_r)
    agc(1).start()
    agc_wait(1)
    unpack(1)
    back = jnp.dot(vis[...], wblk[...], preferred_element_type=F32)
    publish(1, jnp.sum(back * qi[...].astype(F32), axis=1, keepdims=True))
    pace(14)

    load(count_h, count_s, 8).wait()
    row = lax.broadcasted_iota(jnp.int32, (img_all, 1), 0)
    counts = jnp.zeros((img_all, 1), jnp.int32)
    for k in range(ny):
        counts = jnp.where(row // IMG == k, count_s[k], counts)
    live = lax.rem(row, IMG) // PATCH < counts
    inv = lax.rsqrt(collected(0) * per_row + EPS)
    left = jnp.where(live, inv * qi[...].astype(F32), 0.0).astype(BF16)
    pack(0, jnp.dot(vis_t[...], left, preferred_element_type=F32))
    rc(0).start()
    pace(16)
    core_sum(0)
    begin(rx(0), nx)

    mean = collected(1) * per_row
    right = jnp.where(live, (inv * inv * inv * mean) * emb[...].astype(F32), 0.0).astype(BF16)
    pack(1, jnp.dot(vis_t[...], right, preferred_element_type=F32))
    rc(1).start()
    pace(18)
    core_sum(1)
    begin(rx(1), nx)
    pace(19)

    load(text_h, txt, 3).wait()
    sq_t = jnp.zeros((text_rows, 1), F32)
    for s in range(slices):
        rows_t = txt[:, s * tw : (s + 1) * tw].astype(F32)
        sq_t = sq_t + jnp.sum(rows_t * rows_t, axis=1, keepdims=True)
    x_sum(0)
    begin(rz(0), nz)
    pace(21)
    x_sum(1)
    begin(rz(1), nz)
    pace(23)

    rows_f[0, 0:shard, :] = z_sum(0)
    for q in range(packed):
        lhs[:, q * LANES : (q + 1) * LANES] = rows_f[0, pl.ds(q, own_rows, packed), :].astype(BF16)
    term = lhs[:, 0:width]
    for m in range(ny):
        prod = dot_nt(term, qw[m * width : (m + 1) * width, :])
        for q in range(packed):
            rows_f[m, pl.ds(q, own_rows, packed), :] = prod[:, q * LANES : (q + 1) * LANES]
        ty[m] = rows_f[m, 0:shard, :].astype(BF16)
    begin(ty_send, ny)
    pace(pieces)
    each(in_half, text_near)
    first_part = jnp.where(early, in_half, 0)
    each(first_part, text_last)
    second = z_sum(1)
    drain(ty_in, ty_r)
    one_term = ty[y].astype(F32)
    for j in range(ny - 1):
        one_term = one_term + ty_in[j].astype(F32)
    at = lax.rem(lax.broadcasted_iota(jnp.int32, (shard, LANES), 0), packed)
    gain_own = jnp.zeros((shard, LANES), F32)
    for q in range(packed):
        cols = pl.ds(pl.multiple_of(y * width + q * LANES, LANES), LANES)
        gain_own = jnp.where(at == q, gain[:, cols], gain_own)
    proj_o[...] = (gain_own * one_term - second) * (float(nz * nx * 2 * img_all) ** -0.5)
    each(in_half, text_last, first_part)

    cross_t = jnp.sum(cross_f[...], axis=1, keepdims=True)
    inv_t = lax.rsqrt(sq_t * per_row + EPS)
    scale_t = inv_t * inv_t * inv_t * (cross_t * per_row)
    for s in range(slices):
        cols = slice(s * tw, (s + 1) * tw)
        text_o[:, cols] = (inv_t * gtxt[s] - txt[:, cols].astype(F32) * scale_t).astype(BF16)

    drain(sy.at[pl.ds(0, ny - 1)], sy_s)
    for k in (0, 1):
        agz_wait(k, agz_s)
        agx_wait(k, agx_s)
        agc(k).wait_send()
        drain(st_in.at[k], st_s.at[k])
        rc(k).wait_send()
        drain(hx.at[k], rx_s.at[k])
        drain(hz.at[k], rz_s.at[k])
    drain(ty_in, ty_s)
    for way in (0, 1):
        drain(tb.at[way, pl.ds(0, pieces)], ts_s.at[way])


def put_out(text_v, proj_v, text_o, proj_o, sems):
    a = pltpu.make_async_copy(text_v, text_o, sems.at[0])
    b = pltpu.make_async_copy(proj_v, proj_o, sems.at[1])
    a.start()
    b.start()
    a.wait()
    b.wait()


def body(vision_rows, image_count, proj_flat, text_embeds, norm_gain, q_weight, q_grad):
    nz, nx, ny = (lax.axis_size(a) for a in ("dp_0", "dp_1", "mp"))
    total, width = q_weight.shape
    img_all, enc = vision_rows.shape
    text_rows = text_embeds.shape[0]
    shard = proj_flat.shape[0]
    packed = width // LANES
    own_rows = -(-shard // packed // 16) * 16
    near = ny // 2
    slices = 8
    tw = total // slices
    flat_rows = nz * nx * 2 * shard
    live_z = -(-enc * packed // (2 * nx * shard))
    sem = pltpu.SemaphoreType.DMA
    any_space = pl.BlockSpec(memory_space=pl.ANY)
    in_vmem = pl.BlockSpec(memory_space=pltpu.VMEM)
    scratch = [
        pltpu.VMEM((total, width), BF16),
        pltpu.VMEM((img_all, width), BF16),
        pltpu.VMEM((ny, text_rows, width), BF16),
        pltpu.VMEM((img_all, enc), BF16),
        pltpu.VMEM((enc, img_all), BF16),
        pltpu.VMEM((text_rows, total), BF16),
        pltpu.VMEM((1, total), F32),
        pltpu.VMEM((ny, shard, LANES), BF16),
        pltpu.VMEM((ny, own_rows * packed, LANES), F32),
        pltpu.VMEM((own_rows, total), BF16),
        pltpu.VMEM((2, 2, nx, nz, shard, LANES), BF16),
        pltpu.VMEM((flat_rows, LANES), F32),
        pltpu.VMEM((enc, width), BF16),
        pltpu.VMEM((img_all, width), BF16),
        pltpu.VMEM((2, (near + 1) * slices, text_rows, tw), BF16),
        pltpu.VMEM((slices, text_rows, tw), F32),
        pltpu.VMEM((text_rows, LANES), F32),
        pltpu.VMEM((2, 1, img_all), F32),
        pltpu.VMEM((2, ny - 1, 1, img_all), F32),
        pltpu.VMEM((2, 2, nx, nz, shard, LANES), BF16),
        pltpu.VMEM((2, nx, nz, shard, LANES), BF16),
        pltpu.VMEM((2, nx, nz, shard, LANES), BF16),
        pltpu.VMEM((2, nx - 1, live_z, shard, LANES), BF16),
        pltpu.VMEM((2, nz, shard, LANES), BF16),
        pltpu.VMEM((2, nz - 1, shard, LANES), BF16),
        pltpu.VMEM((ny, shard, LANES), BF16),
        pltpu.VMEM((ny - 1, shard, LANES), BF16),
        pltpu.SMEM((ny,), jnp.int32),
        pltpu.SemaphoreType.REGULAR,
        pltpu.SemaphoreType.REGULAR,
        sem((9 + slices // 2,)),
        sem,
        sem,
        *([sem((2,))] * 6),
        sem((2,)),
        sem((2, (near - 1) * slices // 2 + 1 + slices // 2)),
        *([sem((2,))] * 8),
        sem,
        sem,
    ]
    text_v, proj_v = pl.pallas_call(
        functools.partial(kernel, (nz, nx, ny)),
        out_shape=(pltpu.VMEM(text_embeds.shape, BF16), pltpu.VMEM(proj_flat.shape, F32)),
        in_specs=[any_space] * 7,
        out_specs=(in_vmem, in_vmem),
        scratch_shapes=scratch,
        compiler_params=pltpu.CompilerParams(
            collective_id=0,
            has_side_effects=True,
            vmem_limit_bytes=56 * 1024 * 1024,
        ),
        name="step",
    )(vision_rows, image_count, proj_flat, text_embeds, norm_gain.reshape(1, -1), q_weight, q_grad)
    return pl.pallas_call(
        put_out,
        out_shape=(
            jax.ShapeDtypeStruct(text_embeds.shape, BF16),
            jax.ShapeDtypeStruct(proj_flat.shape, F32),
        ),
        in_specs=[in_vmem] * 2,
        out_specs=(any_space, any_space),
        scratch_shapes=[sem((2,))],
        name="put_out",
    )(*(pltpu.with_memory_space_constraint(v, pltpu.VMEM) for v in (text_v, proj_v)))


def solution(mesh):
    finer = Mesh(mesh.devices.reshape(12, 4, 2, mesh.shape["mp"]), ("dp_0", "dp_1", "dp_2", "mp"))
    placed = (P(DP, None), P(DP), P(DP_MP, None), P(DP_MP, None), P(), P(None, "mp"), P(DP, "mp"))
    return jax.shard_map(
        body,
        mesh=finer,
        in_specs=placed,
        out_specs=(P(DP_MP, None), P(DP_MP, None)),
        check_vma=False,
    )
```

time: 94.3 us -> 77.2 us (0.82)
  Pallas kernels: 92.4 us -> 75.6 us
    pallas_call x1, Pallas kernels: 91.5 us -> 74.7 us  [body(): pl.pallas_call(functools.partial(kernel, (nz, nx, ny)), out_shape=(pltpu....]
where the time goes in v3:
time: 77.2 us; the launch traced here: 76.2 us
  Pallas kernels  75.6 us (98%)
    pallas_call x1, Pallas kernels, body(): pl.pallas_call(functools.partial(kernel, (nz, nx, ny)), out_shape=(pltpu....  74.7 us

profile of v3, /device:TPU:1, one launch (start us, length us, event | category | flops | bytes accessed | tf_op | source)
XLA Modules:
  0.0 76.2 jit_solution(2305173061637490538)
XLA Ops:
  0.6 74.7 %step.1 = (bf16[96,4096]{1,0:T(8,128)(2,1)S(1)}, f32[48,128]{1,0:T(8,128)S(1)}) custom-call(bf16[256,1024]{1,0:T(8,128)(2,1)} %vis_h.1, s32[8]{0:T(128)} %count_h.1, bf16[48,128]{1,0:T(8,128)(2,1)} %proj_h.1, bf16[96,4096]{1,0:T(8,128)(2,1)} %text_h.1, f32[1,4096]{1,0:T(1,128)} %bitcast.1, bf16[4096,512]{1,0:T(8,128)(2,1)} %qw_h.1, bf16[1024,512]{1,0:T(8,128)(2,1)} %qg_h.1), custom_call_target="tpu_custom_call" | custom-call | tf_op jit(solution)/shard_map/step/pallas_call | solution.py:675
  75.3 0.9 %put_out.1 = (bf16[96,4096]{1,0:T(8,128)(2,1)}, f32[48,128]{1,0:T(8,128)}) custom-call(bf16[96,4096]{1,0:T(8,128)(2,1)S(1)} %get-tuple-element.4.text_v, f32[48,128]{1,0:T(8,128)S(1)} %get-tuple-element.5.proj_v), custom_call_target="tpu_custom_call" | custom-call | tf_op jit(solution)/shard_map/put_out/pallas_call | solution.py:688

commit v4 on v3

--- a/solution.py
+++ b/solution.py
@@ -105,7 +105,7 @@
     packed = width // LANES
     shard = proj_h.shape[0]
     own_rows = lhs.shape[0]
-    live_z = hx.shape[2]
+    live_z = -(-enc * packed // (2 * nx * shard))
     other = 1 - c
     per_row = 1.0 / total
 
@@ -280,7 +280,7 @@
     steps = (ny - 3) * in_half
     firsts = 2 * in_half
     pieces = firsts + steps
-    ahead = jnp.maximum(LEAD - 3 * z // 4, 0) + jnp.maximum((5 - turn(y)) // 2, 0)
+    ahead = jnp.maximum(LEAD - 3 * z // 4, 0) + jnp.clip((6 - turn(y)) // 2, 0, 2)
     out = [jnp.int32(1), 1]
 
     def pace(n, most=None, times=1, more=0):
@@ -341,25 +341,39 @@
             hs.at[k, other, :, live], hc.at[k, :, live], rc_s.at[k], rc_r.at[k], "dp_2", other
         )
 
-    def rx(k):
-        return lambda j: send(
-            h1.at[k, ring(x + j, nx), pl.ds(0, live_z)],
-            hx.at[k, j - 1],
-            rx_s.at[k],
-            rx_r.at[k],
-            "dp_1",
-            ring(x + j, nx),
-        )
-
-    def rz(k):
-        return lambda j: send(
-            h2.at[k, ring(z + j, nz)],
-            hz.at[k, j - 1],
-            rz_s.at[k],
-            rz_r.at[k],
-            "dp_0",
-            ring(z + j, nz),
-        )
+    side_z = min(2, (nz - 1) // 2)
+    near_z = 2 * side_z + 1
+    runs = (pl.ds(near_z, nz - near_z), pl.ds(0, near_z))
+    FAR, NEAR = 0, 1
+
+    def slot_z(zz):
+        return ring(zz - z + side_z + nz, nz)
+
+    def rx(k, part):
+        def one(j):
+            to = ring(x + j, nx)
+            src, dst = h1.at[k, to, runs[part]], hx.at[k, j - 1, runs[part]]
+            return send(src, dst, rx_s.at[k], rx_r.at[k, part], "dp_1", to)
+
+        begin(one, nx)
+
+    def rz(k, part):
+        def one(off):
+            to = ring(z + off + nz, nz)
+            return send(
+                h2.at[k, off + side_z], hz.at[k, off + side_z], rz_s.at[k], rz_r.at[k], "dp_0", to
+            )
+
+        if part == NEAR:
+            for off in range(side_z, 0, -1):
+                one(off).start()
+                one(-off).start()
+            return
+
+        def by_side(i):
+            one(nz // 2 + jnp.where(lax.rem(i, 2) == 1, (i + 1) // 2, -(i // 2))).start()
+
+        each(nz - near_z, by_side)
 
     def st_send(k):
         return lambda j: send(
@@ -404,26 +418,29 @@
         def one(zz):
             for xx in range(nx):
                 pair = hs[k, c, xx, zz].astype(F32) + hc[k, xx, zz].astype(F32)
-                h1[k, xx, zz] = pair.astype(BF16)
+                h1[k, xx, slot_z(zz)] = pair.astype(BF16)
 
         each(live_z, one)
 
-    def x_sum(k):
-        drain(hx.at[k], rx_r.at[k])
-
-        def one(zz):
-            acc = h1[k, x, zz].astype(F32)
+    def x_sum(k, part):
+        drain(hx.at[k, :, runs[part]], rx_r.at[k, part])
+
+        def one(slot):
+            acc = h1[k, x, slot].astype(F32)
             for j in range(nx - 1):
-                acc = acc + hx[k, j, zz].astype(F32)
-            h2[k, zz] = acc.astype(BF16)
-
-        each(live_z, one)
+                acc = acc + hx[k, j, slot].astype(F32)
+            h2[k, slot] = acc.astype(BF16)
+
+        lo, hi = (near_z, nz) if part == FAR else (0, near_z)
+        each(hi, one, lo)
+        rz(k, part)
 
     def z_sum(k):
-        drain(hz.at[k], rz_r.at[k])
-        acc = h2[k, z].astype(F32)
-        for j in range(nz - 1):
-            acc = acc + hz[k, j].astype(F32)
+        drain(hz.at[k, pl.ds(0, nz - 1)], rz_r.at[k])
+        acc = h2[k, side_z].astype(F32)
+        for slot in range(nz):
+            if slot != side_z:
+                acc = acc + hz[k, slot].astype(F32)
         return acc
 
     def publish(k, column):
@@ -479,7 +496,8 @@
     rows_f[...] = jnp.zeros(rows_f.shape, F32)
     cross_f[...] = jnp.zeros(cross_f.shape, F32)
     for k in (0, 1):
-        h2[k, live_z:] = jnp.zeros((nz - live_z, shard, LANES), BF16)
+        for zz in range(live_z, nz):
+            h1[k, :, slot_z(zz)] = jnp.zeros((nx, shard, LANES), BF16)
     pace(4)
     load(vis_h, vis, 2).wait()
     vis_t[...] = vis[...].T
@@ -513,7 +531,7 @@
     emb[...] = embed
     embed = embed.astype(F32)
     publish(0, jnp.sum(embed * embed, axis=1, keepdims=True))
-    pace(12)
+    pace(13)
 
     agx_wait(1, agx_r)
     agc(1).start()
@@ -535,28 +553,30 @@
     rc(0).start()
     pace(16)
     core_sum(0)
-    begin(rx(0), nx)
+    rx(0, FAR)
+    rx(0, NEAR)
+    pace(17)
 
     mean = collected(1) * per_row
     right = jnp.where(live, (inv * inv * inv * mean) * emb[...].astype(F32), 0.0).astype(BF16)
     pack(1, jnp.dot(vis_t[...], right, preferred_element_type=F32))
     rc(1).start()
-    pace(18)
+    pace(19)
     core_sum(1)
-    begin(rx(1), nx)
-    pace(19)
+    rx(1, FAR)
+    rx(1, NEAR)
+    x_sum(0, FAR)
+    pace(20)
 
     load(text_h, txt, 3).wait()
     sq_t = jnp.zeros((text_rows, 1), F32)
     for s in range(slices):
         rows_t = txt[:, s * tw : (s + 1) * tw].astype(F32)
         sq_t = sq_t + jnp.sum(rows_t * rows_t, axis=1, keepdims=True)
-    x_sum(0)
-    begin(rz(0), nz)
-    pace(21)
-    x_sum(1)
-    begin(rz(1), nz)
-    pace(23)
+    x_sum(0, NEAR)
+    pace(22)
+    x_sum(1, FAR)
+    pace(24, pieces - 2)
 
     rows_f[0, 0:shard, :] = z_sum(0)
     for q in range(packed):
@@ -568,6 +588,7 @@
             rows_f[m, pl.ds(q, own_rows, packed), :] = prod[:, q * LANES : (q + 1) * LANES]
         ty[m] = rows_f[m, 0:shard, :].astype(BF16)
     begin(ty_send, ny)
+    x_sum(1, NEAR)
     pace(pieces)
     each(in_half, text_near)
     first_part = jnp.where(early, in_half, 0)
@@ -600,7 +621,7 @@
         drain(st_in.at[k], st_s.at[k])
         rc(k).wait_send()
         drain(hx.at[k], rx_s.at[k])
-        drain(hz.at[k], rz_s.at[k])
+        drain(hz.at[k, pl.ds(0, nz - 1)], rz_s.at[k])
     drain(ty_in, ty_s)
     for way in (0, 1):
         drain(tb.at[way, pl.ds(0, pieces)], ts_s.at[way])
@@ -627,7 +648,6 @@
     slices = 8
     tw = total // slices
     flat_rows = nz * nx * 2 * shard
-    live_z = -(-enc * packed // (2 * nx * shard))
     sem = pltpu.SemaphoreType.DMA
     any_space = pl.BlockSpec(memory_space=pl.ANY)
     in_vmem = pl.BlockSpec(memory_space=pltpu.VMEM)
@@ -654,9 +674,9 @@
         pltpu.VMEM((2, 2, nx, nz, shard, LANES), BF16),
         pltpu.VMEM((2, nx, nz, shard, LANES), BF16),
         pltpu.VMEM((2, nx, nz, shard, LANES), BF16),
-        pltpu.VMEM((2, nx - 1, live_z, shard, LANES), BF16),
+        pltpu.VMEM((2, nx - 1, nz, shard, LANES), BF16),
         pltpu.VMEM((2, nz, shard, LANES), BF16),
-        pltpu.VMEM((2, nz - 1, shard, LANES), BF16),
+        pltpu.VMEM((2, nz, shard, LANES), BF16),
         pltpu.VMEM((ny, shard, LANES), BF16),
         pltpu.VMEM((ny - 1, shard, LANES), BF16),
         pltpu.SMEM((ny,), jnp.int32),
@@ -668,7 +688,9 @@
         *([sem((2,))] * 6),
         sem((2,)),
         sem((2, (near - 1) * slices // 2 + 1 + slices // 2)),
-        *([sem((2,))] * 8),
+        *([sem((2,))] * 5),
+        sem((2, 2)),
+        *([sem((2,))] * 2),
         sem,
         sem,
     ]

time: 77.2 us -> 75.2 us (0.974)
  Pallas kernels: 75.6 us -> 74 us
    pallas_call x1, Pallas kernels: 74.7 us -> 73.1 us  [body(): pl.pallas_call(functools.partial(kernel, (nz, nx, ny)), out_shape=(pltpu....]
where the time goes in v4:
time: 75.2 us; the launch traced here: 74.6 us
  Pallas kernels  74 us (98%)
    pallas_call x1, Pallas kernels, body(): pl.pallas_call(functools.partial(kernel, (nz, nx, ny)), out_shape=(pltpu....  73.1 us

profile of v4, /device:TPU:1, one launch (start us, length us, event | category | flops | bytes accessed | tf_op | source)
XLA Modules:
  0.0 74.6 jit_solution(17049644222021441364)
XLA Ops:
  0.6 73.1 %step.1 = (bf16[96,4096]{1,0:T(8,128)(2,1)S(1)}, f32[48,128]{1,0:T(8,128)S(1)}) custom-call(bf16[256,1024]{1,0:T(8,128)(2,1)} %vis_h.1, s32[8]{0:T(128)} %count_h.1, bf16[48,128]{1,0:T(8,128)(2,1)} %proj_h.1, bf16[96,4096]{1,0:T(8,128)(2,1)} %text_h.1, f32[1,4096]{1,0:T(1,128)} %bitcast.1, bf16[4096,512]{1,0:T(8,128)(2,1)} %qw_h.1, bf16[1024,512]{1,0:T(8,128)(2,1)} %qg_h.1), custom_call_target="tpu_custom_call" | custom-call | tf_op jit(solution)/shard_map/step/pallas_call | solution.py:697
  73.7 0.9 %put_out.1 = (bf16[96,4096]{1,0:T(8,128)(2,1)}, f32[48,128]{1,0:T(8,128)}) custom-call(bf16[96,4096]{1,0:T(8,128)(2,1)S(1)} %get-tuple-element.4.text_v, f32[48,128]{1,0:T(8,128)S(1)} %get-tuple-element.5.proj_v), custom_call_target="tpu_custom_call" | custom-call | tf_op jit(solution)/shard_map/put_out/pallas_call | solution.py:710

commit v5 on v0

v5 whole, which is shorter than its diff:
```python
import functools

import jax
import jax.numpy as jnp
from jax import lax
from jax.experimental import pallas as pl
from jax.experimental.pallas import tpu as pltpu
from jax.sharding import Mesh
from jax.sharding import PartitionSpec as P

IMG_MAX = 4
PATCH = 8
IMG = IMG_MAX * PATCH
LANES = 128
DP = ("dp_0", "dp_1", "dp_2")
DP_MP = ("dp_0", "dp_1", "dp_2", "mp")
EPS = 1e-05
LEAD = 7
SLACK = 143
EARLY = 3
MESH = pl.DeviceIdType.MESH
F32 = jnp.float32
BF16 = jnp.bfloat16


def dot_nt(a, b):
    return lax.dot_general(a, b, (((1,), (1,)), ((), ())), preferred_element_type=F32)


def kernel(
    sizes,
    vis_h,
    count_h,
    proj_h,
    text_h,
    gain_h,
    qw_h,
    qg_h,
    text_o,
    proj_o,
    qw,
    qi,
    qt,
    vis,
    vis_t,
    txt,
    gain,
    sy,
    rows_f,
    lhs,
    ag,
    flat,
    wblk,
    emb,
    tb,
    gtxt,
    cross_f,
    sq_f,
    st,
    st_in,
    hs,
    hc,
    h1,
    hx,
    h2,
    hz,
    ty,
    ty_in,
    count_s,
    ts_s,
    ts_r,
):
    nz, nx, ny = sizes
    text_rows, total = txt.shape
    near = ny // 2
    slices = gtxt.shape[0]
    in_half = slices // 2
    tw = tb.shape[3]
    per_row = 1.0 / total
    pieces = 2 * in_half + (ny - 3) * in_half
    mid_sems = (near - 1) * slices // 2

    def drain(ref, sem):
        pltpu.make_async_copy(ref, ref, sem).wait()

    def each(n, act, lo=0):
        def one(k, carry):
            act(k)
            return carry

        lax.fori_loop(lo, n, one, 0)

    def arrival(way, d, h, k):
        mid = ((d - 1) * slices + h * in_half + k) // 2
        end = mid_sems + jnp.where(h == way, 1 + k, 0)
        return ts_r.at[way, jnp.where(d > 0, mid, end)]

    def text_last(k):
        for h in (0, 1):
            s = h * in_half + k
            drain(tb.at[h, 0], arrival(h, 0, h, k))
            cols = pl.ds(pl.multiple_of(s * tw, LANES), tw)
            g = (gtxt[s] + tb[h, s].astype(F32)) * gain[:, cols]
            gtxt[s] = g
            prod = g * txt[:, cols].astype(F32)
            for q in range(tw // LANES):
                cross_f[...] += prod[:, q * LANES : (q + 1) * LANES]

    def work(
        in_sem,
        y_sem,
        load_sem,
        sy_s,
        sy_r,
        agz_s,
        agz_r,
        agx_s,
        agx_r,
        agc_s,
        agc_r,
        st_s,
        st_r,
        rc_s,
        rc_r,
        rx_s,
        rx_r,
        rz_s,
        rz_r,
        ty_s,
        ty_r,
    ):
        z = lax.axis_index("dp_0")
        x = lax.axis_index("dp_1")
        c = lax.axis_index("dp_2")
        y = lax.axis_index("mp")
        width = qw.shape[1]
        enc = vis.shape[1]
        img_all = qi.shape[0]
        packed = width // LANES
        shard = proj_h.shape[0]
        own_rows = lhs.shape[0]
        live_z = -(-enc * packed // (2 * nx * shard))
        other = 1 - c

        def ring(i, n):
            return lax.rem(i, n)

        def begin(make, n):
            def one(i, carry):
                side = jnp.where(lax.rem(i, 2) == 1, (i + 1) // 2, -(i // 2))
                make(n // 2 + side).start()
                return carry

            lax.fori_loop(0, n - 1, one, 0)

        def send(src, dst, send_sem, recv_sem, axis, index):
            return pltpu.make_async_remote_copy(
                src_ref=src,
                dst_ref=dst,
                send_sem=send_sem,
                recv_sem=recv_sem,
                device_id={axis: index},
                device_id_type=MESH,
            )

        def load(src, dst, i):
            return pltpu.make_async_copy(src, dst, load_sem.at[i])

        rows_each = IMG + text_rows

        def text_in(k, i):
            base = pl.multiple_of(k * rows_each + IMG, 16)
            return load(qg_h.at[pl.ds(base, text_rows)], qt.at[k], i)

        def img_in(k):
            base = pl.multiple_of(k * rows_each, 16)
            to = qi.at[pl.ds(pl.multiple_of(k * IMG, 16), IMG)]
            return load(qg_h.at[pl.ds(base, IMG)], to, 7)

        def slice_in(s):
            cols = pl.ds(pl.multiple_of(s * tw, tw), tw)
            return load(qw_h.at[cols], qw.at[cols], 9 + lax.rem(s, in_half))

        def pair_wait(i):
            drain(qw.at[pl.ds(0, 2 * tw)], load_sem.at[9 + i])

        slice_in(0).start()
        text_in(ring(y + near, ny), 5).start()
        slice_in(in_half).start()
        load(proj_h, ag.at[0, c, x, z], 0).start()
        load(proj_h, sy.at[y], 1).start()

        barrier = pltpu.get_barrier_semaphore()

        def tell(what, axis, index):
            pl.semaphore_signal(what, inc=1, device_id={axis: index}, device_id_type=MESH)

        corner_z = ((x == 0) & (y == 0) & (c == 0)).astype(jnp.int32)
        corner_x = ((z == 0) & (y == 0) & (c == 0)).astype(jnp.int32)
        corner_y = ((z == 0) & (x == 0) & (c == 0)).astype(jnp.int32)
        rank_z = ring(z + nz - corner_z, nz)
        rank_x = ring(x + nx - corner_x, nx)

        def tell_z(what):
            return lambda r: tell(what, "dp_0", ring(r + corner_z, nz))

        def tell_x(what):
            return lambda r: tell(what, "dp_1", ring(r + corner_x, nx))

        def turn(v):
            place = jnp.where(v < near, v, ny + near - 1 - v)
            place = jnp.where(place == near, near - 1, jnp.where(place == near - 1, near, place))
            return ring(place + ny - corner_y, ny)

        def awaits(a, b, j):
            return (turn(b) < turn(a)) | (j == 1) | (j == ny - 1)

        y_now = jnp.int32(0)
        for j in range(1, ny):
            v = ring(y + j, ny)
            y_now = y_now + awaits(y, v, j).astype(jnp.int32)

            @pl.when(awaits(v, y, j))
            def _(v=v):
                tell(barrier, "mp", v)

        each(nz, tell_z(barrier), rank_z + 1)
        each(nx, tell_x(barrier), rank_x + 1)

        @pl.when(c == 1)
        def _():
            tell(barrier, "dp_2", other)

        def next_slices(i):
            slice_in(i).start()
            slice_in(in_half + i).start()

        each(in_half, next_slices, 1)
        each(ny, lambda j: text_in(ring(y + near + j, ny), 6).start(), 1)
        load(gain_h, gain, 4).start()
        load(vis_h, vis, 2).start()
        each(ny, lambda k: img_in(k).start())
        load(text_h, txt, 3).start()
        load(count_h, count_s, 8).start()

        def owner_of(way, d):
            return ring(y + d, ny) if way == 0 else ring(y + ny - d, ny)

        def text_dot(owner, s):
            cols = qw[pl.ds(pl.multiple_of(s * tw, tw), tw), :]
            return dot_nt(qt[owner], cols)

        def text_send(way, d, h, k):
            s = h * in_half + k
            return send(
                tb.at[way, d * slices + s],
                tb.at[way, (d - 1) * slices + s],
                ts_s.at[way],
                arrival(way, d - 1, h, k),
                "mp",
                ring(y + 1, ny) if way == 0 else ring(y + ny - 1, ny),
            )

        def text_first(i):
            far = i < in_half
            k = lax.rem(i, in_half)
            for way in (0, 1):
                h = jnp.where(far, way, 1 - way)
                d = jnp.where(far, near, near - 1)
                s = h * in_half + k
                tb[way, d * slices + s] = text_dot(owner_of(way, d), s).astype(BF16)
                text_send(way, d, h, k).start()

        def text_next_first(i):
            @pl.when(i < in_half)
            def _():
                pair_wait(i)

            text_first(i)

        def text_relay(n):
            u = n // in_half
            k = lax.rem(n, in_half)
            d = near - 1 - (u + 1) // 2
            for way in (0, 1):
                h = lax.rem(u + way, 2)
                s = h * in_half + k
                slot = d * slices + s
                mine = text_dot(owner_of(way, d), s)

                @pl.when(lax.rem(k, 2) == 0)
                def _(way=way, d=d, h=h, k=k):
                    drain(tb.at[way, pl.ds(0, 2)], arrival(way, d, h, k))

                tb[way, slot] = (mine + tb[way, slot].astype(F32)).astype(BF16)
                text_send(way, d, h, k).start()

        steps = (ny - 3) * in_half
        firsts = 2 * in_half
        place = jnp.where(y < near, y, ny + near - 1 - y)
        begins = jnp.where(z < 7, 35 + 14 * z, 110 + 3 * z)
        begins += jnp.where(y < near, 6 * y - 30, 3 * (place - near) - 10)
        begins += jnp.where(x < 2, 5 * x - 10, 0) - 4 * c
        ahead = jnp.clip((SLACK - begins) // 21, 0, LEAD)
        out = [jnp.int32(1), 1]

        def pace(n, most=None, times=1, more=0):
            most = min(n + LEAD if most is None else most, pieces)
            upto = jnp.minimum(n + times * ahead + more, most)
            upto = jnp.maximum(upto, out[0])
            if out[1] < firsts:
                each(jnp.minimum(upto, firsts), text_next_first, jnp.minimum(out[0], firsts))
            if most > firsts:
                each(jnp.maximum(upto, firsts) - firsts, text_relay, jnp.maximum(out[0], firsts) - firsts)
            out[0], out[1] = upto, max(out[1], min(n, pieces))

        def text_near(k):
            @pl.when(k == 0)
            def _():
                for way in (0, 1):
                    drain(tb.at[way, pl.ds(0, in_half)], arrival(way, 0, 1 - way, 0))

            for h in (0, 1):
                s = h * in_half + k
                gtxt[s] = text_dot(y, s) + tb[1 - h, s].astype(F32)

        def agz(k):
            ref = ag.at[k, c, x, z]
            return lambda j: send(ref, ref, agz_s, agz_r.at[k], "dp_0", ring(z + j, nz))

        def agx(k):
            ref = ag.at[k, c, x, pl.ds(0, live_z)]
            return lambda j: send(ref, ref, agx_s, agx_r.at[k], "dp_1", ring(x + j, nx))

        def agc(k):
            ref = ag.at[k, c]
            return send(ref, ref, agc_s, agc_r.at[k], "dp_2", other)

        def agz_wait(k):
            drain(ag.at[0, 0, 0, pl.ds(0, nz - 1)], agz_r.at[k])

        def agx_wait(k):
            drain(ag.at[0, 0, pl.ds(0, nx - 1), pl.ds(0, live_z)], agx_r.at[k])

        def agc_wait(k):
            drain(ag.at[0, 0], agc_r.at[k])

        def rc(k):
            live = pl.ds(0, live_z)
            return send(
                hs.at[k, other, :, live], hc.at[k, :, live], rc_s, rc_r.at[k], "dp_2", other
            )

        side_z = min(2, (nz - 1) // 2)
        near_z = 2 * side_z + 1
        runs = (pl.ds(near_z, nz - near_z), pl.ds(0, near_z))
        FAR, NEAR = 0, 1

        def slot_z(zz):
            return ring(zz - z + side_z + nz, nz)

        def rx(k, part):
            def one(j):
                to = ring(x + j, nx)
                src, dst = h1.at[k, to, runs[part]], hx.at[k, j - 1, runs[part]]
                return send(src, dst, rx_s, rx_r.at[k, part], "dp_1", to)

            begin(one, nx)

        def rz(k, part):
            def one(off):
                to = ring(z + off + nz, nz)
                return send(
                    h2.at[k, off + side_z], hz.at[k, off + side_z], rz_s, rz_r.at[k], "dp_0", to
                )

            if part == NEAR:
                for off in range(side_z, 0, -1):
                    one(off).start()
                    one(-off).start()
                return

            def by_side(i):
                one(nz // 2 + jnp.where(lax.rem(i, 2) == 1, (i + 1) // 2, -(i // 2))).start()

            each(nz - near_z, by_side)

        def st_send(k):
            return lambda j: send(
                st.at[k], st_in.at[k, j - 1], st_s, st_r.at[k], "mp", ring(y + j, ny)
            )

        def sy_send(j):
            return send(sy.at[y], sy.at[y], sy_s, sy_r, "mp", ring(y + j, ny))

        def ty_send(j):
            to = ring(y + j, ny)
            return send(ty.at[to], ty_in.at[j - 1], ty_s, ty_r, "mp", to)

        def place(zz, r):
            return pl.ds(pl.multiple_of((zz * 2 * nx + r) * shard, 16), shard)

        def unpack(k):
            def one(zz):
                for r in range(2 * nx):
                    flat[place(zz, r), :] = ag[k, r % 2, r // 2, zz].astype(F32)

            each(live_z, one)
            for q in range(packed):
                wblk[:, q * LANES : (q + 1) * LANES] = flat[pl.ds(q, enc, packed), :].astype(BF16)

        def pack(k, block):
            for q in range(packed):
                flat[pl.ds(q, enc, packed), :] = block[:, q * LANES : (q + 1) * LANES]
            end = live_z * 2 * nx * shard
            if end > enc * packed:
                flat[enc * packed : end, :] = jnp.zeros((end - enc * packed, LANES), F32)

            def one(zz):
                for r in range(2 * nx):
                    hs[k, r % 2, r // 2, zz] = flat[place(zz, r), :].astype(BF16)

            each(live_z, one)

        def core_sum(k):
            rc(k).wait_recv()

            def one(zz):
                for xx in range(nx):
                    pair = hs[k, c, xx, zz].astype(F32) + hc[k, xx, zz].astype(F32)
                    h1[k, xx, slot_z(zz)] = pair.astype(BF16)

            each(live_z, one)

        def x_sum(k, part):
            drain(hx.at[k, :, runs[part]], rx_r.at[k, part])

            def one(slot):
                acc = h1[k, x, slot].astype(F32)
                for j in range(nx - 1):
                    acc = acc + hx[k, j, slot].astype(F32)
                h2[k, slot] = acc.astype(BF16)

            lo, hi = (near_z, nz) if part == FAR else (0, near_z)
            each(hi, one, lo)
            rz(k, part)

        def z_sum(k):
            drain(hz.at[k, pl.ds(0, nz - 1)], rz_r.at[k])
            acc = h2[k, side_z].astype(F32)
            for slot in range(nz):
                if slot != side_z:
                    acc = acc + hz[k, slot].astype(F32)
            return acc

        def publish(k, column):
            wide = jnp.broadcast_to(column, (img_all, LANES))
            st[k] = wide.T[0:1, :]
            begin(st_send(k), ny)

        def collected(k):
            drain(st_in.at[k], st_r.at[k])
            row = st[k]
            for j in range(ny - 1):
                row = row + st_in[k, j]
            return jnp.broadcast_to(row, (LANES, img_all)).T[:, 0:1]

        def text_ahead(way):
            tb[way, near * slices + way * in_half] = text_dot(owner_of(way, near), way * in_half).astype(BF16)

        pair_wait(0)
        text_in(ring(y + near, ny), 5).wait()
        text_ahead(0)
        pl.semaphore_wait(barrier, y_now + rank_z + rank_x + other)
        each(rank_z, tell_z(in_sem))
        text_send(0, near, 0, 0).start()
        text_ahead(1)
        text_send(1, near, 1, 0).start()
        each(rank_x, tell_x(in_sem))
        load(proj_h, sy.at[y], 1).wait()

        @pl.when(c == 0)
        def _():
            tell(in_sem, "dp_2", other)

        for j in range(1, ny):
            v = ring(y + j, ny)

            @pl.when(jnp.logical_not(awaits(v, y, j)))
            def _(v=v):
                tell(y_sem, "mp", v)

        load(proj_h, ag.at[0, c, x, z], 0).wait()
        drain(qt.at[pl.ds(0, ny - 1)], load_sem.at[6])

        early = z < EARLY
        pace(1, 3, 0, (ny - 1 - turn(y)) // 3)

        @pl.when(y_now < ny - 1)
        def _():
            pl.semaphore_wait(y_sem, ny - 1 - y_now)

        begin(sy_send, ny)
        pace(1, firsts + 2, 2)
        rest = (nz - 1 - rank_z) + (nx - 1 - rank_x) + c

        @pl.when(rest > 0)
        def _():
            pl.semaphore_wait(in_sem, rest)

        begin(agz(0), nz)
        rows_f[...] = jnp.zeros(rows_f.shape, F32)
        cross_f[...] = jnp.zeros(cross_f.shape, F32)
        for k in (0, 1):
            for zz in range(live_z, nz):
                h1[k, :, slot_z(zz)] = jnp.zeros((nx, shard, LANES), BF16)
        pace(4)
        load(vis_h, vis, 2).wait()
        vis_t[...] = vis[...].T
        pace(6)
        agz_wait(0)
        begin(agx(0), nx)

        load(gain_h, gain, 4).wait()
        drain(sy.at[pl.ds(0, ny - 1)], sy_r)
        for m in range(ny):
            rows_f[m, 0:shard, :] = sy[m].astype(F32)
            for q in range(packed):
                cols = slice(m * width + q * LANES, m * width + (q + 1) * LANES)
                piece = rows_f[m, pl.ds(q, own_rows, packed), :] * gain[:, cols]
                lhs[:, cols] = piece.astype(BF16)
        prod = jnp.dot(lhs[...], qw[...], preferred_element_type=F32)
        for q in range(packed):
            rows_f[0, pl.ds(q, own_rows, packed), :] = prod[:, q * LANES : (q + 1) * LANES]
        ag[1, c, x, z] = rows_f[0, 0:shard, :].astype(BF16)
        begin(agz(1), nz)
        pace(9)
        agx_wait(0)
        agc(0).start()

        drain(qi, load_sem.at[7])
        agz_wait(1)
        begin(agx(1), nx)
        agc_wait(0)
        unpack(0)
        embed = jnp.dot(vis[...], wblk[...], preferred_element_type=F32).astype(BF16)
        emb[...] = embed
        embed = embed.astype(F32)
        publish(0, jnp.sum(embed * embed, axis=1, keepdims=True))
        pace(13)

        agx_wait(1)
        agc(1).start()
        agc_wait(1)
        unpack(1)
        back = jnp.dot(vis[...], wblk[...], preferred_element_type=F32)
        publish(1, jnp.sum(back * qi[...].astype(F32), axis=1, keepdims=True))
        pace(14)

        load(count_h, count_s, 8).wait()
        row = lax.broadcasted_iota(jnp.int32, (img_all, 1), 0)
        counts = jnp.zeros((img_all, 1), jnp.int32)
        for k in range(ny):
            counts = jnp.where(row // IMG == k, count_s[k], counts)
        live = lax.rem(row, IMG) // PATCH < counts
        inv = lax.rsqrt(collected(0) * per_row + EPS)
        left = jnp.where(live, inv * qi[...].astype(F32), 0.0).astype(BF16)
        pack(0, jnp.dot(vis_t[...], left, preferred_element_type=F32))
        rc(0).start()
        pace(16)
        core_sum(0)
        rx(0, FAR)
        rx(0, NEAR)
        pace(17)

        mean = collected(1) * per_row
        right = jnp.where(live, (inv * inv * inv * mean) * emb[...].astype(F32), 0.0).astype(BF16)
        pack(1, jnp.dot(vis_t[...], right, preferred_element_type=F32))
        rc(1).start()
        pace(19)
        core_sum(1)
        rx(1, FAR)
        rx(1, NEAR)
        x_sum(0, FAR)
        pace(20)

        load(text_h, txt, 3).wait()
        sq_t = jnp.zeros((text_rows, 1), F32)
        for s in range(slices):
            rows_t = txt[:, s * tw : (s + 1) * tw].astype(F32)
            sq_t = sq_t + jnp.sum(rows_t * rows_t, axis=1, keepdims=True)
        sq_f[...] = jnp.broadcast_to(sq_t, sq_f.shape)
        x_sum(0, NEAR)
        pace(22)
        x_sum(1, FAR)
        pace(24, pieces - 2)

        rows_f[0, 0:shard, :] = z_sum(0)
        for q in range(packed):
            lhs[:, q * LANES : (q + 1) * LANES] = rows_f[0, pl.ds(q, own_rows, packed), :].astype(BF16)
        term = lhs[:, 0:width]
        for m in range(ny):
            prod = dot_nt(term, qw[m * width : (m + 1) * width, :])
            for q in range(packed):
                rows_f[m, pl.ds(q, own_rows, packed), :] = prod[:, q * LANES : (q + 1) * LANES]
            ty[m] = rows_f[m, 0:shard, :].astype(BF16)
        begin(ty_send, ny)
        x_sum(1, NEAR)
        pace(pieces)
        each(in_half, text_near)
        first_part = jnp.where(early, in_half, 0)
        each(first_part, text_last)
        second = z_sum(1)
        drain(ty_in, ty_r)
        one_term = ty[y].astype(F32)
        for j in range(ny - 1):
            one_term = one_term + ty_in[j].astype(F32)
        at = lax.rem(lax.broadcasted_iota(jnp.int32, (shard, LANES), 0), packed)
        gain_own = jnp.zeros((shard, LANES), F32)
        for q in range(packed):
            cols = pl.ds(pl.multiple_of(y * width + q * LANES, LANES), LANES)
            gain_own = jnp.where(at == q, gain[:, cols], gain_own)
        proj_o[...] = (gain_own * one_term - second) * (float(nz * nx * 2 * img_all) ** -0.5)
        drain(sy.at[pl.ds(0, ny - 1)], sy_s)
        drain(ag.at[0, 0, pl.ds(0, 2), pl.ds(0, nz - 1)], agz_s)
        drain(ag.at[:, 0, pl.ds(0, nx - 1), pl.ds(0, live_z)], agx_s)
        drain(ag.at[0], agc_s)
        drain(st_in, st_s)
        drain(hc.at[:, :, pl.ds(0, live_z)], rc_s)
        drain(hx, rx_s)
        drain(hz.at[:, pl.ds(0, nz - 1)], rz_s)
        drain(ty_in, ty_s)

    sem = pltpu.SemaphoreType.DMA
    pl.run_scoped(
        work,
        pltpu.SemaphoreType.REGULAR,
        pltpu.SemaphoreType.REGULAR,
        sem((9 + in_half,)),
        sem,
        sem,
        *([sem, sem((2,))] * 3),
        *([sem, sem((2,))] * 2),
        sem,
        sem((2, 2)),
        sem,
        sem((2,)),
        sem,
        sem,
    )

    each(in_half, text_last, jnp.where(lax.axis_index("dp_0") < EARLY, in_half, 0))

    cross_t = jnp.sum(cross_f[...], axis=1, keepdims=True)
    inv_t = lax.rsqrt(sq_f[:, 0:1] * per_row + EPS)
    scale_t = inv_t * inv_t * inv_t * (cross_t * per_row)
    for s in range(slices):
        cols = slice(s * tw, (s + 1) * tw)
        text_o[:, cols] = (inv_t * gtxt[s] - txt[:, cols].astype(F32) * scale_t).astype(BF16)

    for way in (0, 1):
        drain(tb.at[way, pl.ds(0, pieces)], ts_s.at[way])


def put_out(text_v, proj_v, text_o, proj_o, sems):
    a = pltpu.make_async_copy(text_v, text_o, sems.at[0])
    b = pltpu.make_async_copy(proj_v, proj_o, sems.at[1])
    a.start()
    b.start()
    a.wait()
    b.wait()


def body(vision_rows, image_count, proj_flat, text_embeds, norm_gain, q_weight, q_grad):
    nz, nx, ny = (lax.axis_size(a) for a in ("dp_0", "dp_1", "mp"))
    total, width = q_weight.shape
    img_all, enc = vision_rows.shape
    text_rows = text_embeds.shape[0]
    shard = proj_flat.shape[0]
    packed = width // LANES
    own_rows = -(-shard // packed // 16) * 16
    near = ny // 2
    slices = 8
    tw = total // slices
    flat_rows = nz * nx * 2 * shard
    sem = pltpu.SemaphoreType.DMA
    any_space = pl.BlockSpec(memory_space=pl.ANY)
    in_vmem = pl.BlockSpec(memory_space=pltpu.VMEM)
    scratch = [
        pltpu.VMEM((total, width), BF16),
        pltpu.VMEM((img_all, width), BF16),
        pltpu.VMEM((ny, text_rows, width), BF16),
        pltpu.VMEM((img_all, enc), BF16),
        pltpu.VMEM((enc, img_all), BF16),
        pltpu.VMEM((text_rows, total), BF16),
        pltpu.VMEM((1, total), F32),
        pltpu.VMEM((ny, shard, LANES), BF16),
        pltpu.VMEM((ny, own_rows * packed, LANES), F32),
        pltpu.VMEM((own_rows, total), BF16),
        pltpu.VMEM((2, 2, nx, nz, shard, LANES), BF16),
        pltpu.VMEM((flat_rows, LANES), F32),
        pltpu.VMEM((enc, width), BF16),
        pltpu.VMEM((img_all, width), BF16),
        pltpu.VMEM((2, (near + 1) * slices, text_rows, tw), BF16),
        pltpu.VMEM((slices, text_rows, tw), F32),
        pltpu.VMEM((text_rows, LANES), F32),
        pltpu.VMEM((text_rows, LANES), F32),
        pltpu.VMEM((2, 1, img_all), F32),
        pltpu.VMEM((2, ny - 1, 1, img_all), F32),
        pltpu.VMEM((2, 2, nx, nz, shard, LANES), BF16),
        pltpu.VMEM((2, nx, nz, shard, LANES), BF16),
        pltpu.VMEM((2, nx, nz, shard, LANES), BF16),
        pltpu.VMEM((2, nx - 1, nz, shard, LANES), BF16),
        pltpu.VMEM((2, nz, shard, LANES), BF16),
        pltpu.VMEM((2, nz, shard, LANES), BF16),
        pltpu.VMEM((ny, shard, LANES), BF16),
        pltpu.VMEM((ny - 1, shard, LANES), BF16),
        pltpu.SMEM((ny,), jnp.int32),
        sem((2,)),
        sem((2, (near - 1) * slices // 2 + 1 + slices // 2)),
    ]
    text_v, proj_v = pl.pallas_call(
        functools.partial(kernel, (nz, nx, ny)),
        out_shape=(pltpu.VMEM(text_embeds.shape, BF16), pltpu.VMEM(proj_flat.shape, F32)),
        in_specs=[any_space] * 7,
        out_specs=(in_vmem, in_vmem),
        scratch_shapes=scratch,
        compiler_params=pltpu.CompilerParams(
            collective_id=0,
            has_side_effects=True,
            vmem_limit_bytes=56 * 1024 * 1024,
        ),
        name="step",
    )(vision_rows, image_count, proj_flat, text_embeds, norm_gain.reshape(1, -1), q_weight, q_grad)
    return pl.pallas_call(
        put_out,
        out_shape=(
            jax.ShapeDtypeStruct(text_embeds.shape, BF16),
            jax.ShapeDtypeStruct(proj_flat.shape, F32),
        ),
        in_specs=[in_vmem] * 2,
        out_specs=(any_space, any_space),
        scratch_shapes=[sem((2,))],
        name="put_out",
    )(*(pltpu.with_memory_space_constraint(v, pltpu.VMEM) for v in (text_v, proj_v)))


def solution(mesh):
    finer = Mesh(mesh.devices.reshape(12, 4, 2, mesh.shape["mp"]), ("dp_0", "dp_1", "dp_2", "mp"))
    placed = (P(DP, None), P(DP), P(DP_MP, None), P(DP_MP, None), P(), P(None, "mp"), P(DP, "mp"))
    return jax.shard_map(
        body,
        mesh=finer,
        in_specs=placed,
        out_specs=(P(DP_MP, None), P(DP_MP, None)),
        check_vma=False,
    )
```

time: 300 us -> 74.7 us (0.25)
  the two profiles are of different devices: /device:TPU:2 before, /device:TPU:1 now
where the time goes in v5:
time: 74.7 us; the launch traced here: 74.4 us
  Pallas kernels  73.8 us (99%)
    pallas_call x1, Pallas kernels, body(): pl.pallas_call(functools.partial(kernel, (nz, nx, ny)), out_shape=(pltpu....  72.9 us

profile of v5, /device:TPU:1, one launch (start us, length us, event | category | flops | bytes accessed | tf_op | source)
XLA Modules:
  0.0 74.4 jit_solution(17399677388612742339)
XLA Ops:
  0.6 72.9 %step.1 = (bf16[96,4096]{1,0:T(8,128)(2,1)S(1)}, f32[48,128]{1,0:T(8,128)S(1)}) custom-call(bf16[256,1024]{1,0:T(8,128)(2,1)} %vis_h.1, s32[8]{0:T(128)} %count_h.1, bf16[48,128]{1,0:T(8,128)(2,1)} %proj_h.1, bf16[96,4096]{1,0:T(8,128)(2,1)} %text_h.1, f32[1,4096]{1,0:T(1,128)} %bitcast.1, bf16[4096,512]{1,0:T(8,128)(2,1)} %qw_h.1, bf16[1024,512]{1,0:T(8,128)(2,1)} %qg_h.1), custom_call_target="tpu_custom_call" | custom-call | tf_op jit(solution)/shard_map/step/pallas_call | solution.py:722
  73.5 0.9 %put_out.1 = (bf16[96,4096]{1,0:T(8,128)(2,1)}, f32[48,128]{1,0:T(8,128)}) custom-call(bf16[96,4096]{1,0:T(8,128)(2,1)S(1)} %get-tuple-element.4.text_v, f32[48,128]{1,0:T(8,128)S(1)} %get-tuple-element.5.proj_v), custom_call_target="tpu_custom_call" | custom-call | tf_op jit(solution)/shard_map/put_out/pallas_call | solution.py:735

commit v6 on v5

--- a/solution.py
+++ b/solution.py
@@ -16,7 +16,7 @@
 DP_MP = ("dp_0", "dp_1", "dp_2", "mp")
 EPS = 1e-05
 LEAD = 7
-SLACK = 143
+SLACK = 148
 EARLY = 3
 MESH = pl.DeviceIdType.MESH
 F32 = jnp.float32
@@ -39,6 +39,7 @@
     text_o,
     proj_o,
     qw,
+    qw_t,
     qi,
     qt,
     vis,
@@ -246,9 +247,18 @@
         def owner_of(way, d):
             return ring(y + d, ny) if way == 0 else ring(y + ny - d, ny)
 
-        def text_dot(owner, s):
-            cols = qw[pl.ds(pl.multiple_of(s * tw, tw), tw), :]
-            return dot_nt(qt[owner], cols)
+        def text_dot(owner, s, turned=False):
+            cols = pl.ds(pl.multiple_of(s * tw, tw), tw)
+            if turned:
+                return jnp.dot(qt[owner], qw_t[:, cols], preferred_element_type=F32)
+            return dot_nt(qt[owner], qw[cols, :])
+
+        def turn_weight():
+            def one(s):
+                cols = pl.ds(pl.multiple_of(s * tw, tw), tw)
+                qw_t[:, cols] = qw[cols, :].T
+
+            each(slices, one)
 
         def text_send(way, d, h, k):
             s = h * in_half + k
@@ -278,7 +288,7 @@
 
             text_first(i)
 
-        def text_relay(n):
+        def text_relay(n, turned):
             u = n // in_half
             k = lax.rem(n, in_half)
             d = near - 1 - (u + 1) // 2
@@ -286,7 +296,7 @@
                 h = lax.rem(u + way, 2)
                 s = h * in_half + k
                 slot = d * slices + s
-                mine = text_dot(owner_of(way, d), s)
+                mine = text_dot(owner_of(way, d), s, turned)
 
                 @pl.when(lax.rem(k, 2) == 0)
                 def _(way=way, d=d, h=h, k=k):
@@ -300,18 +310,18 @@
         place = jnp.where(y < near, y, ny + near - 1 - y)
         begins = jnp.where(z < 7, 35 + 14 * z, 110 + 3 * z)
         begins += jnp.where(y < near, 6 * y - 30, 3 * (place - near) - 10)
-        begins += jnp.where(x < 2, 5 * x - 10, 0) - 4 * c
+        begins += jnp.where(x < 2, 5 * x - 10, 0) + c
         ahead = jnp.clip((SLACK - begins) // 21, 0, LEAD)
         out = [jnp.int32(1), 1]
 
-        def pace(n, most=None, times=1, more=0):
+        def pace(n, most=None, times=1, more=0, turned=True):
             most = min(n + LEAD if most is None else most, pieces)
             upto = jnp.minimum(n + times * ahead + more, most)
             upto = jnp.maximum(upto, out[0])
             if out[1] < firsts:
                 each(jnp.minimum(upto, firsts), text_next_first, jnp.minimum(out[0], firsts))
             if most > firsts:
-                each(jnp.maximum(upto, firsts) - firsts, text_relay, jnp.maximum(out[0], firsts) - firsts)
+                each(jnp.maximum(upto, firsts) - firsts, lambda n: text_relay(n, turned), jnp.maximum(out[0], firsts) - firsts)
             out[0], out[1] = upto, max(out[1], min(n, pieces))
 
         def text_near(k):
@@ -322,7 +332,7 @@
 
             for h in (0, 1):
                 s = h * in_half + k
-                gtxt[s] = text_dot(y, s) + tb[1 - h, s].astype(F32)
+                gtxt[s] = text_dot(y, s, True) + tb[1 - h, s].astype(F32)
 
         def agz(k):
             ref = ag.at[k, c, x, z]
@@ -494,14 +504,14 @@
         drain(qt.at[pl.ds(0, ny - 1)], load_sem.at[6])
 
         early = z < EARLY
-        pace(1, 3, 0, (ny - 1 - turn(y)) // 3)
+        pace(1, 3, 0, (ny - 1 - turn(y)) // 3, False)
 
         @pl.when(y_now < ny - 1)
         def _():
             pl.semaphore_wait(y_sem, ny - 1 - y_now)
 
         begin(sy_send, ny)
-        pace(1, firsts + 2, 2)
+        pace(1, firsts + 2, 2, turned=False)
         rest = (nz - 1 - rank_z) + (nx - 1 - rank_x) + c
 
         @pl.when(rest > 0)
@@ -514,10 +524,11 @@
         for k in (0, 1):
             for zz in range(live_z, nz):
                 h1[k, :, slot_z(zz)] = jnp.zeros((nx, shard, LANES), BF16)
-        pace(4)
+        pace(4, turned=False)
         load(vis_h, vis, 2).wait()
         vis_t[...] = vis[...].T
-        pace(6)
+        pace(6, turned=False)
+        turn_weight()
         agz_wait(0)
         begin(agx(0), nx)
 
@@ -600,7 +611,7 @@
             lhs[:, q * LANES : (q + 1) * LANES] = rows_f[0, pl.ds(q, own_rows, packed), :].astype(BF16)
         term = lhs[:, 0:width]
         for m in range(ny):
-            prod = dot_nt(term, qw[m * width : (m + 1) * width, :])
+            prod = jnp.dot(term, qw_t[:, m * width : (m + 1) * width], preferred_element_type=F32)
             for q in range(packed):
                 rows_f[m, pl.ds(q, own_rows, packed), :] = prod[:, q * LANES : (q + 1) * LANES]
             ty[m] = rows_f[m, 0:shard, :].astype(BF16)
@@ -688,6 +699,7 @@
     in_vmem = pl.BlockSpec(memory_space=pltpu.VMEM)
     scratch = [
         pltpu.VMEM((total, width), BF16),
+        pltpu.VMEM((width, total), BF16),
         pltpu.VMEM((img_all, width), BF16),
         pltpu.VMEM((ny, text_rows, width), BF16),
         pltpu.VMEM((img_all, enc), BF16),

time: 74.7 us -> 74.6 us (level)
  no operation moved by 1% of the time
where the time goes in v6:
time: 74.6 us; the launch traced here: 74.4 us
  Pallas kernels  73.8 us (99%)
    pallas_call x1, Pallas kernels, body(): pl.pallas_call(functools.partial(kernel, (nz, nx, ny)), out_shape=(pltpu....  72.9 us

profile of v6, /device:TPU:1, one launch (start us, length us, event | category | flops | bytes accessed | tf_op | source)
XLA Modules:
  0.0 74.4 jit_solution(8018512487655171146)
XLA Ops:
  0.6 72.9 %step.1 = (bf16[96,4096]{1,0:T(8,128)(2,1)S(1)}, f32[48,128]{1,0:T(8,128)S(1)}) custom-call(bf16[256,1024]{1,0:T(8,128)(2,1)} %vis_h.1, s32[8]{0:T(128)} %count_h.1, bf16[48,128]{1,0:T(8,128)(2,1)} %proj_h.1, bf16[96,4096]{1,0:T(8,128)(2,1)} %text_h.1, f32[1,4096]{1,0:T(1,128)} %bitcast.1, bf16[4096,512]{1,0:T(8,128)(2,1)} %qw_h.1, bf16[1024,512]{1,0:T(8,128)(2,1)} %qg_h.1), custom_call_target="tpu_custom_call" | custom-call | tf_op jit(solution)/shard_map/step/pallas_call | solution.py:734
  73.5 0.9 %put_out.1 = (bf16[96,4096]{1,0:T(8,128)(2,1)}, f32[48,128]{1,0:T(8,128)}) custom-call(bf16[96,4096]{1,0:T(8,128)(2,1)S(1)} %get-tuple-element.4.text_v, f32[48,128]{1,0:T(8,128)S(1)} %get-tuple-element.5.proj_v), custom_call_target="tpu_custom_call" | custom-call | tf_op jit(solution)/shard_map/put_out/pallas_call | solution.py:747

commit v7 on v5

--- a/solution.py
+++ b/solution.py
@@ -177,16 +177,16 @@
             to = qi.at[pl.ds(pl.multiple_of(k * IMG, 16), IMG)]
             return load(qg_h.at[pl.ds(base, IMG)], to, 7)
 
-        def slice_in(s):
+        def slice_in(s, own=None):
             cols = pl.ds(pl.multiple_of(s * tw, tw), tw)
-            return load(qw_h.at[cols], qw.at[cols], 9 + lax.rem(s, in_half))
+            return load(qw_h.at[cols], qw.at[cols], 9 + lax.rem(s, in_half) if own is None else own)
 
         def pair_wait(i):
             drain(qw.at[pl.ds(0, 2 * tw)], load_sem.at[9 + i])
 
         slice_in(0).start()
         text_in(ring(y + near, ny), 5).start()
-        slice_in(in_half).start()
+        slice_in(in_half, 9 + in_half).start()
         load(proj_h, ag.at[0, c, x, z], 0).start()
         load(proj_h, sy.at[y], 1).start()
 
@@ -468,14 +468,28 @@
         def text_ahead(way):
             tb[way, near * slices + way * in_half] = text_dot(owner_of(way, near), way * in_half).astype(BF16)
 
-        pair_wait(0)
+        last = y == near
         text_in(ring(y + near, ny), 5).wait()
-        text_ahead(0)
+
+        def ahead_of(way):
+            slice_in(way * in_half, 9 + way * in_half).wait()
+            text_ahead(way)
+
+        def in_turn(first):
+            def then():
+                for way in (first, 1 - first):
+                    if way != first:
+                        ahead_of(way)
+                    text_send(way, near, way, 0).start()
+
+            return then
+
+        pl.when(last)(lambda: ahead_of(1))
+        pl.when(jnp.logical_not(last))(lambda: ahead_of(0))
         pl.semaphore_wait(barrier, y_now + rank_z + rank_x + other)
         each(rank_z, tell_z(in_sem))
-        text_send(0, near, 0, 0).start()
-        text_ahead(1)
-        text_send(1, near, 1, 0).start()
+        pl.when(last)(in_turn(1))
+        pl.when(jnp.logical_not(last))(in_turn(0))
         each(rank_x, tell_x(in_sem))
         load(proj_h, sy.at[y], 1).wait()
 
@@ -636,7 +650,7 @@
         work,
         pltpu.SemaphoreType.REGULAR,
         pltpu.SemaphoreType.REGULAR,
-        sem((9 + in_half,)),
+        sem((10 + in_half,)),
         sem,
         sem,
         *([sem, sem((2,))] * 3),

time: 74.7 us -> 74.8 us (level)
  no operation moved by 1% of the time
where the time goes in v7:
time: 74.8 us; the launch traced here: 74.4 us
  Pallas kernels  73.8 us (99%)
    pallas_call x1, Pallas kernels, body(): pl.pallas_call(functools.partial(kernel, (nz, nx, ny)), out_shape=(pltpu....  72.9 us

profile of v7, /device:TPU:1, one launch (start us, length us, event | category | flops | bytes accessed | tf_op | source)
XLA Modules:
  0.0 74.4 jit_solution(15609428647746866582)
XLA Ops:
  0.6 72.9 %step.1 = (bf16[96,4096]{1,0:T(8,128)(2,1)S(1)}, f32[48,128]{1,0:T(8,128)S(1)}) custom-call(bf16[256,1024]{1,0:T(8,128)(2,1)} %vis_h.1, s32[8]{0:T(128)} %count_h.1, bf16[48,128]{1,0:T(8,128)(2,1)} %proj_h.1, bf16[96,4096]{1,0:T(8,128)(2,1)} %text_h.1, f32[1,4096]{1,0:T(1,128)} %bitcast.1, bf16[4096,512]{1,0:T(8,128)(2,1)} %qw_h.1, bf16[1024,512]{1,0:T(8,128)(2,1)} %qg_h.1), custom_call_target="tpu_custom_call" | custom-call | tf_op jit(solution)/shard_map/step/pallas_call | solution.py:736
  73.5 0.9 %put_out.1 = (bf16[96,4096]{1,0:T(8,128)(2,1)}, f32[48,128]{1,0:T(8,128)}) custom-call(bf16[96,4096]{1,0:T(8,128)(2,1)S(1)} %get-tuple-element.4.text_v, f32[48,128]{1,0:T(8,128)S(1)} %get-tuple-element.5.proj_v), custom_call_target="tpu_custom_call" | custom-call | tf_op jit(solution)/shard_map/put_out/pallas_call | solution.py:749
